TPU v7x, 32 devices: a whole 2x2x4 slice. The times are simulated.
32 devices in a mesh: expert: 8 (over z, y), vocab: 4 (over x, core).
Axes of the slice: x: 2, y: 2, z: 4, core: 2. Of those that a mesh axis runs over, the one named last changes fastest.
Arguments:
- tokens: bfloat16 [2048, 2048], P('expert'), may hold values from -6 to 6
- teacher_expert: int32 [2048, 1], P('expert'), may hold values from 0 to 3
- student_expert: int32 [2048, 1], P('expert'), may hold values from 0 to 3
- priority: int32 [8, 256], P('expert'), may hold values from 0 to 255, each once within a row
- expert_in: bfloat16 [8, 2048, 8192], P('expert', None, 'vocab'), may hold values from -0.125 to 0.125
- expert_out: bfloat16 [8, 8192, 2048], P('expert', 'vocab'), may hold values from -0.0625 to 0.0625
- teacher_gain: float32 [2048], replicated, may hold values from 0.1 to 1.9
- student_gain: float32 [2048], replicated, may hold values from 0.1 to 1.9
- teacher_head: bfloat16 [8192, 2048], P(('vocab', 'expert')), may hold values from -4 to 4
- student_head: bfloat16 [8192, 2048], P(('vocab', 'expert')), may hold values from -4 to 4
Outputs:
- token_kl: float32 [2048], P('expert')
Inputs may be any that keep to these rules, and one draw needn't show every extreme that they name: Each row of priority holds every number of 0 to 255 once.
All inputs are finite; a program needn't handle non-finite values.
Results may differ from a plain program's by a relative error of at most 0.0032.
Values may be sent and summed in bfloat16 or wider, within the bound.
No kernel may reach another device: no remote copies, remote signals or barrier semaphores. Data moves between devices by JAX's collectives and lax.ppermute only.
A program may use at most 128 MiB of HBM per device.

v0:
```python
import jax
import jax.numpy as jnp
from jax import lax
from jax.experimental import pallas as pl
from jax.experimental.pallas import tpu as pltpu
from jax.sharding import PartitionSpec as P


BOTH = ("expert", "vocab")


def slot_ranks(expert, ranking):
    same_expert = expert[:, None] == expert[None, :]
    before = ranking[None, :] < ranking[:, None]
    return jnp.sum(jnp.logical_and(same_expert, before).astype(jnp.int32), axis=1)


def ffn(rows, weight_in, weight_out):
    hidden = jax.nn.gelu(
        jnp.dot(rows, weight_in, preferred_element_type=jnp.float32)
    ).astype(jnp.bfloat16)
    return jnp.dot(hidden, weight_out, preferred_element_type=jnp.float32).astype(jnp.bfloat16)


def set_of(w):
    return (w & 1) | ((w >> 2) << 1), (w >> 1) & 1


def finish(flip, places, gains, tokens, pools, t_shards, s_shards):
    width = gains.shape[-1]
    piece = tokens[0].shape[0]
    rows = piece * len(tokens)
    tile = min(rows, 256)
    height = pools[0].shape[1]
    reach = height * len(pools)
    entries = t_shards[0].shape[0]
    span = entries * len(t_shards)
    shards = list(t_shards) + list(s_shards)
    counts = (len(tokens), len(pools), len(shards))

    def kernel(flip_ref, place_ref, gain_ref, *refs):
        token_in, refs = refs[: counts[0]], refs[counts[0] :]
        pool_in, refs = refs[: counts[1]], refs[counts[1] :]
        head_in, refs = refs[: counts[2]], refs[counts[2] :]
        out_ref, token, pool, head, normed, logits, token_sem, pool_sem, head_sem = refs
        copies = {}
        for branch in range(2):
            for i in range(counts[1]):
                copies["pool", branch, i] = pltpu.make_async_copy(
                    pool_in[i].at[flip_ref[0] ^ branch],
                    pool.at[branch, pl.ds(i * height, height)],
                    pool_sem.at[branch, i],
                )
                copies["pool", branch, i].start()
            if branch == 0:
                for i in range(counts[0]):
                    copies["token", i] = pltpu.make_async_copy(
                        token_in[i], token.at[pl.ds(i * piece, piece)], token_sem.at[i]
                    )
                    copies["token", i].start()
        for i in range(counts[2]):
            copies["head", i] = pltpu.make_async_copy(head_in[i], head.at[i], head_sem.at[i])
            copies["head", i].start()
        for branch in range(2):
            for i in range(counts[1]):
                copies["pool", branch, i].wait()
            if branch == 0:
                for i in range(counts[0]):
                    copies["token", i].wait()
            for t in range(rows // tile):
                here = pl.ds(t * tile, tile)
                number = lax.broadcasted_iota(jnp.int32, (tile, reach), 1)
                picked = jnp.where(number == place_ref[branch, here], 1.0, 0.0)
                total = token[here, :].astype(jnp.float32) + jnp.dot(
                    picked.astype(jnp.bfloat16), pool[branch], preferred_element_type=jnp.float32
                )
                mean = jnp.mean(total * total, axis=-1, keepdims=True)
                scaled = total * lax.rsqrt(mean + 1e-05) * gain_ref[branch]
                normed[branch, here, :] = scaled.astype(jnp.bfloat16)
        for i in range(counts[2]):
            copies["head", i].wait()
            branch, part = divmod(i, len(t_shards))
            logits[branch, :, part * entries : (part + 1) * entries] = lax.dot_general(
                normed[branch],
                head[i],
                (((1,), (1,)), ((), ())),
                preferred_element_type=jnp.float32,
            )
        for t in range(rows // tile):
            here = pl.ds(t * tile, tile)
            teacher, student = logits[0, here, :], logits[1, here, :]
            tp = jnp.max(teacher, axis=1, keepdims=True)
            sp = jnp.max(student, axis=1, keepdims=True)
            te = jnp.exp(teacher - tp)
            columns = [
                tp,
                jnp.sum(te, axis=1, keepdims=True),
                jnp.sum(te * (teacher - student), axis=1, keepdims=True),
                sp,
                jnp.sum(jnp.exp(student - sp), axis=1, keepdims=True),
            ]
            lane = lax.broadcasted_iota(jnp.int32, (tile, 128), 1)
            table = jnp.zeros((tile, 128), jnp.float32)
            for i, column in enumerate(columns):
                table = jnp.where(lane == i, column, table)
            out_ref[:, t * tile : (t + 1) * tile] = table.T[:8]

    return pl.pallas_call(
        kernel,
        in_specs=[
            pl.BlockSpec(memory_space=pltpu.SMEM),
            pl.BlockSpec(memory_space=pltpu.VMEM),
            pl.BlockSpec(memory_space=pltpu.VMEM),
        ]
        + [pl.BlockSpec(memory_space=pl.ANY)] * sum(counts),
        out_specs=pl.BlockSpec(memory_space=pltpu.VMEM),
        out_shape=jax.ShapeDtypeStruct((8, rows), jnp.float32),
        scratch_shapes=[
            pltpu.VMEM((rows, width), jnp.bfloat16),
            pltpu.VMEM((2, reach, width), jnp.bfloat16),
            pltpu.VMEM((len(shards), entries, width), jnp.bfloat16),
            pltpu.VMEM((2, rows, width), jnp.bfloat16),
            pltpu.VMEM((2, rows, span), jnp.float32),
            pltpu.SemaphoreType.DMA((counts[0],)),
            pltpu.SemaphoreType.DMA((2, counts[1])),
            pltpu.SemaphoreType.DMA((counts[2],)),
        ],
        name="finish",
    )(flip, places, gains, *tokens, *pools, *shards)


def local(
    tokens,
    teacher_expert,
    student_expert,
    priority,
    expert_in,
    expert_out,
    teacher_gain,
    student_gain,
    teacher_head,
    student_head,
):
    count, width = tokens.shape
    En = lax.axis_size("expert")
    Vn = lax.axis_size("vocab")
    J = En // Vn
    H = En // 4
    X = Vn // 2
    cap = 3 * count // En
    hc = cap // 2
    hcnt = count // 2
    e = lax.axis_index("expert")
    v = lax.axis_index("vocab")
    x, c = v // 2, v % 2
    zh, zl, y = e // 4, (e // 2) % 2, e % 2

    def by_expert(array, move):
        return lax.ppermute(array, "expert", [(s, move(s)) for s in range(En)])

    def by_vocab(array, move):
        return lax.ppermute(array, "vocab", [(s, move(s)) for s in range(Vn)])

    def by_both(array, move):
        perm = []
        for s in range(En):
            for u in range(Vn):
                de, dv = move(s, u)
                perm.append((s * Vn + u, de * Vn + dv))
        return lax.ppermute(array, BOTH, perm)

    other_core = lambda array: by_vocab(array, lambda u: u ^ 1)

    ranking = priority[0]
    codes = []
    for expert in (teacher_expert[:, 0], student_expert[:, 0]):
        rank = slot_ranks(expert, ranking)
        codes.append(jnp.where(rank < cap, expert * cap + rank, -1))

    group_rows = jnp.arange(En * hc, dtype=jnp.int32)[:, None]
    chosen = jnp.zeros((En * hc, count), jnp.bool_)
    for lane, code in enumerate(codes):
        slot = code % cap
        target = (2 * (code // cap) + lane) ^ e
        mine = jnp.logical_and(code >= 0, slot // hc == c)
        place = jnp.where(mine, target * hc + slot % hc, -1)
        chosen = jnp.logical_or(chosen, group_rows == place[None, :])
    outgoing = jnp.dot(chosen.astype(jnp.bfloat16), tokens, preferred_element_type=jnp.float32)
    outgoing = outgoing.astype(jnp.bfloat16).reshape(En, hc, width)

    order = [m1 * 2 + (xi & 1) + ((xi >> 1) << 2) for m1 in range(2) for xi in range(X)]
    arrived = {0: outgoing[0]}
    for g in range(1, En):
        arrived[g] = by_expert(outgoing[g], lambda s: s ^ g)

    t_shards, s_shards = [teacher_head], [student_head]
    for d in range(1, X):
        t_shards.append(by_vocab(teacher_head, lambda u: u ^ (2 * d)))
        s_shards.append(by_vocab(student_head, lambda u: u ^ (2 * d)))
    s_far = by_expert(student_head, lambda s: s ^ 2)
    t_far = by_expert(teacher_head, lambda s: s ^ 2)
    t_diag = [by_expert(t_shards[d], lambda s: s ^ 2) for d in range(1, X)]
    s_diag = [by_vocab(s_far, lambda u: u ^ (2 * d)) for d in range(1, X)]
    t_shards += [t_far] + t_diag
    s_shards += [s_far] + s_diag

    def set_route(rho):
        def move(s, u):
            i = (s // Vn) ^ rho
            q = i * Vn + u
            xd, zld = set_of(s % Vn)
            return (q >> 2) * 4 + zld * 2 + ((q >> 1) & 1), 2 * xd + (q & 1)

        return move

    half_tokens = lax.dynamic_slice_in_dim(tokens, c * hcnt, hcnt, 0)
    numbers = [f(code) for code in codes for f in (lambda a: a // cap, lambda a: a % cap)]
    numbers = jnp.concatenate(numbers).astype(jnp.bfloat16)
    tail = -(-numbers.size // (16 * width)) * 16
    numbers = jnp.pad(numbers, (0, tail * width - numbers.size)).reshape(tail, width)
    parcel = jnp.concatenate([half_tokens, numbers])
    parcels = [by_both(parcel, set_route(rho)) for rho in range(J)]
    set_tokens = [parcel[:hcnt] for parcel in parcels]
    set_tokens += [other_core(array) for array in set_tokens]
    numbers = [parcel[hcnt:].reshape(-1)[: 4 * count] for parcel in parcels]
    numbers = jnp.stack(numbers).astype(jnp.int32).reshape(J, 2, 2, 2, hcnt)
    numbers = jnp.where(c == 0, numbers, numbers[:, :, :, ::-1])
    set_codes = jnp.transpose(numbers, (1, 2, 3, 0, 4)).reshape(2, 2, 2 * J * hcnt)

    weight_in = expert_in[0]
    weight_out = expert_out[0]
    xe, _ = set_of(e % Vn)
    pools = []
    for r in range(J):
        own = jnp.stack([arrived[r * Vn + m] for m in order]).reshape(Vn * hc, width)
        rows = jnp.concatenate([own, other_core(own)], axis=0)
        partial = ffn(rows, weight_in, weight_out).reshape(2, 2, X, hc, width)
        kept_side = zl ^ c
        sent = lax.dynamic_index_in_dim(partial, 1 - kept_side, 1, keepdims=False)
        kept = lax.dynamic_index_in_dim(partial, kept_side, 1, keepdims=False)
        got = other_core(sent)
        summed = kept.astype(jnp.float32) + got[::-1].astype(jnp.float32)
        total = lax.dynamic_index_in_dim(summed, xe ^ x, 1, keepdims=False)
        narrow = summed.astype(jnp.bfloat16)
        for d in range(1, X):
            part = lax.dynamic_index_in_dim(narrow, xe ^ x ^ d, 1, keepdims=False)
            part = by_vocab(part, lambda u: u ^ (2 * d))
            total = total + part.astype(jnp.float32)
        reduced = total.astype(jnp.bfloat16).reshape(cap, width)
        mine, crossed = [], []
        for q in range(H):

            def spread(s, u):
                return ((s // 4) ^ q) * 4 + (u % 2) * 2 + s % 2, (u // 2) * 2 + (s // 2) % 2

            mine.append(by_both(reduced, spread))
            crossed.append(by_expert(mine[-1], lambda s: s ^ 1))
        mine = jnp.stack(mine + crossed).reshape(2, H * cap, width)
        pools += [mine, other_core(mine)]

    me = ((zh * 2 + y) * 2 + c) // Vn
    block_j = me ^ (jnp.arange(2 * J * hcnt, dtype=jnp.int32) // hcnt % J)
    places = []
    for lane in range(2):
        chosen_expert, slot = set_codes[lane]
        source = 2 * chosen_expert + lane
        place = (block_j ^ (source // Vn)) * 2 + ((source // 2 % 2) ^ c)
        place = place * H + ((source // 4) ^ zh)
        place = place * cap + ((slot // hc) ^ zl) * hc + slot % hc
        places.append(jnp.where(chosen_expert >= 0, place, -1))
    stats = finish(
        jnp.reshape(y, (1,)).astype(jnp.int32),
        jnp.stack(places)[:, :, None],
        jnp.stack([teacher_gain, student_gain])[:, None, :],
        set_tokens,
        pools,
        t_shards,
        s_shards,
    )

    def merge(parts, axis):
        tp, tt, tw, sp, st = [lax.index_in_dim(parts, i, axis + 1, keepdims=False) for i in range(5)]
        tpm = jnp.max(tp, axis=axis, keepdims=True)
        spm = jnp.max(sp, axis=axis, keepdims=True)
        tr, sr = jnp.exp(tp - tpm), jnp.exp(sp - spm)
        return (
            jnp.squeeze(tpm, axis),
            jnp.sum(tt * tr, axis=axis),
            jnp.sum(tw * tr, axis=axis),
            jnp.squeeze(spm, axis),
            jnp.sum(st * sr, axis=axis),
        )

    everyone = lax.all_gather(stats, "vocab", axis=0).reshape(X, 2, 8, 2, J, hcnt)
    aligned = jnp.stack([everyone[:, 0], everyone[:, 1, :, ::-1]], axis=1)
    by_x = jnp.stack(merge(aligned, 1), axis=1).reshape(X, 5, 2, J, hcnt)
    neutral = jnp.array([-1e30, 0.0, 0.0, -1e30, 0.0], jnp.float32)[:, None, None]
    letters = []
    for b in range(En):
        xb, zb = set_of(b % Vn)
        letter = lax.dynamic_index_in_dim(by_x[xb], me ^ (b // Vn), 2, keepdims=False)
        letters.append(jnp.where(zl == zb, letter, neutral))
    mail = lax.all_to_all(jnp.stack(letters), "expert", split_axis=0, concat_axis=0, tiled=True)
    tp, tt, tw, sp, st = merge(mail, 0)
    kl = tw / tt - tp - jnp.log(tt) + sp + jnp.log(st)
    return kl.reshape(count)


def solution(mesh):
    in_specs = (
        P("expert", None),
        P("expert", None),
        P("expert", None),
        P("expert", None),
        P("expert", None, "vocab"),
        P("expert", "vocab", None),
        P(),
        P(),
        P(("vocab", "expert"), None),
        P(("vocab", "expert"), None),
    )
    out_specs = P("expert")

    return jax.shard_map(local, mesh=mesh, in_specs=in_specs, out_specs=out_specs, check_vma=False)
```

profile of v0, /device:TPU:0, one launch (start us, length us, event | category | flops | bytes accessed | tf_op | source)
XLA Modules:
  0.0 279.9 jit_solution(11264128243505134379)
XLA Ops:
  2.6 4.1 %collective-permute-start.15 = (bf16[48,2048]{1,0:T(8,128)(2,1)S(1)}, bf16[48,2048]{1,0:T(8,128)(2,1)S(1)}, u32[]{:S(2)}, u32[]{:S(2)}) collective-permute-start(bf16[48,2048]{1,0:T(8,128)(2,1)S(1)} %get-tuple-element.21), channel_id=1, source_target_pairs={{0,16},{4,20},{8,24},{12,28},{16,0},{20,4},{24,8},{28,12},{1,17},{... | collective-permute-start | bytes 589832 | tf_op jit(solution)/shard_map/ppermute | solution.py:159
  8.0 3.6 %collective-permute-start.17 = (bf16[48,2048]{1,0:T(8,128)(2,1)S(1)}, bf16[48,2048]{1,0:T(8,128)(2,1)S(1)}, u32[]{:S(2)}, u32[]{:S(2)}) collective-permute-start(bf16[48,2048]{1,0:T(8,128)(2,1)S(1)} %get-tuple-element.23), channel_id=1, source_target_pairs={{0,24},{4,28},{8,16},{12,20},{16,8},{20,12},{24,0},{28,4},{1,25},{... | collective-permute-start | bytes 589832 | tf_op jit(solution)/shard_map/ppermute | solution.py:159
  11.6 17.7 %collective-permute-done.15 = bf16[48,2048]{1,0:T(8,128)(2,1)S(1)} collective-permute-done((bf16[48,2048]{1,0:T(8,128)(2,1)S(1)}, bf16[48,2048]{1,0:T(8,128)(2,1)S(1)}, u32[]{:S(2)}, u32[]{:S(2)}) %collective-permute-start.15) | collective-permute-done | bytes 196640 | tf_op jit(solution)/shard_map/ppermute | solution.py:159
  29.4 5.5 %collective-permute-done.16 = bf16[48,2048]{1,0:T(8,128)(2,1)S(1)} collective-permute-done((bf16[48,2048]{1,0:T(8,128)(2,1)S(1)}, bf16[48,2048]{1,0:T(8,128)(2,1)S(1)}, u32[]{:S(2)}, u32[]{:S(2)}) %collective-permute-start.16) | collective-permute-done | bytes 196640 | tf_op jit(solution)/shard_map/ppermute | solution.py:159
  35.3 8.3 %collective-permute-start.5 = (bf16[48,2048]{1,0:T(8,128)(2,1)S(1)}, bf16[48,2048]{1,0:T(8,128)(2,1)S(1)}, u32[]{:S(2)}, u32[]{:S(2)}) collective-permute-start(bf16[48,2048]{1,0:T(8,128)(2,1)S(1)} %get-tuple-element.26), channel_id=1, source_target_pairs={{0,8},{4,12},{8,0},{12,4},{16,24},{20,28},{24,16},{28,20},{1,9},{5... | collective-permute-start | bytes 589832 | tf_op jit(solution)/shard_map/ppermute | solution.py:159
  44.5 4.9 %collective-permute-done.5 = bf16[48,2048]{1,0:T(8,128)(2,1)S(1)} collective-permute-done((bf16[48,2048]{1,0:T(8,128)(2,1)S(1)}, bf16[48,2048]{1,0:T(8,128)(2,1)S(1)}, u32[]{:S(2)}, u32[]{:S(2)}) %collective-permute-start.5) | collective-permute-done | bytes 196640 | tf_op jit(solution)/shard_map/ppermute | solution.py:159
  49.4 4.5 %collective-permute-done.6 = bf16[48,2048]{1,0:T(8,128)(2,1)S(1)} collective-permute-done((bf16[48,2048]{1,0:T(8,128)(2,1)S(1)}, bf16[48,2048]{1,0:T(8,128)(2,1)S(1)}, u32[]{:S(2)}, u32[]{:S(2)}) %collective-permute-start.6) | collective-permute-done | bytes 196640 | tf_op jit(solution)/shard_map/ppermute | solution.py:159
  54.8 12.7 %fusion.27 = bf16[384,2048]{1,0:T(8,128)(2,1)S(1)} fusion(bf16[1,2048,2048]{2,1,0:T(8,128)(2,1)} %param.16, bf16[1,2048,2048]{2,1,0:T(8,128)(2,1)} %param.15, bf16[192,2048]{1,0:T(8,128)(2,1)} %collective-permute-done.19, bf16[192,2048]{1,0:T(8,128)(2,1)S(1)} %bitcast.182), kind=kOutput, calls=%fused_computation.27 | convolution fusion | flops 6453460992 | bytes 19922944 | tf_op jit(solution)/shard_map/dot_general | solution.py:22
  69.1 13.0 %fusion.24 = bf16[384,2048]{1,0:T(8,128)(2,1)S(1)} fusion(bf16[1,2048,2048]{2,1,0:T(8,128)(2,1)} %param.16, bf16[1,2048,2048]{2,1,0:T(8,128)(2,1)} %param.15, bf16[192,2048]{1,0:T(8,128)(2,1)} %collective-permute-done.7, bf16[192,2048]{1,0:T(8,128)(2,1)} %bitcast.18), kind=kOutput, calls=%fused_computation.26 | convolution fusion | flops 6453460992 | bytes 19922944 | tf_op jit(solution)/shard_map/dot_general | solution.py:22
  91.7 19.5 %collective-permute-done.21 = bf16[2,48,2048]{2,1,0:T(8,128)(2,1)S(1)} collective-permute-done((bf16[2,48,2048]{2,1,0:T(8,128)(2,1)S(1)}, bf16[2,48,2048]{2,1,0:T(8,128)(2,1)S(1)}, u32[]{:S(2)}, u32[]{:S(2)}) %collective-permute-start.21) | collective-permute-done | bytes 393248 | tf_op jit(solution)/shard_map/ppermute | solution.py:162
  112.7 3.6 %collective-permute-start.23 = (bf16[96,2048]{1,0:T(8,128)(2,1)S(1)}, bf16[96,2048]{1,0:T(8,128)(2,1)}, u32[]{:S(2)}, u32[]{:S(2)}) collective-permute-start(bf16[96,2048]{1,0:T(8,128)(2,1)S(1)} %bitcast.192), channel_id=1, source_target_pairs={{0,16},{1,24},{2,18},{3,26},{4,20},{5,28},{6,22},{7,30},{8,17},{9,... | collective-permute-start | bytes 1179656 | tf_op jit(solution)/shard_map/ppermute | solution.py:170
  119.8 3.7 %collective-permute-start.11 = (bf16[96,2048]{1,0:T(8,128)(2,1)S(1)}, bf16[96,2048]{1,0:T(8,128)(2,1)S(1)}, u32[]{:S(2)}, u32[]{:S(2)}) collective-permute-start(bf16[96,2048]{1,0:T(8,128)(2,1)S(1)} %bitcast.190), channel_id=1, source_target_pairs={{0,16},{1,24},{2,18},{3,26},{4,20},{5,28},{6,22},{7,30},{8,17},{9,... | collective-permute-start | bytes 1179656 | tf_op jit(solution)/shard_map/ppermute | solution.py:170
  124.0 13.0 %collective-permute-done.23 = bf16[96,2048]{1,0:T(8,128)(2,1)} collective-permute-done((bf16[96,2048]{1,0:T(8,128)(2,1)S(1)}, bf16[96,2048]{1,0:T(8,128)(2,1)}, u32[]{:S(2)}, u32[]{:S(2)}) %collective-permute-start.23) | collective-permute-done | bytes 393248 | tf_op jit(solution)/shard_map/ppermute | solution.py:170
  140.6 8.9 %collective-permute-done.11 = bf16[96,2048]{1,0:T(8,128)(2,1)S(1)} collective-permute-done((bf16[96,2048]{1,0:T(8,128)(2,1)S(1)}, bf16[96,2048]{1,0:T(8,128)(2,1)S(1)}, u32[]{:S(2)}, u32[]{:S(2)}) %collective-permute-start.11) | collective-permute-done | bytes 393248 | tf_op jit(solution)/shard_map/ppermute | solution.py:170
  150.5 2.7 collective-permute-start.28
  153.2 3.5 %collective-permute-done.12 = bf16[96,2048]{1,0:T(8,128)(2,1)S(1)} collective-permute-done((bf16[96,2048]{1,0:T(8,128)(2,1)S(1)}, bf16[96,2048]{1,0:T(8,128)(2,1)S(1)}, u32[]{:S(2)}, u32[]{:S(2)}) %collective-permute-start.12) | collective-permute-done | bytes 393248 | tf_op jit(solution)/shard_map/ppermute | solution.py:159
  157.7 3.2 %collective-permute-done.13 = bf16[96,2048]{1,0:T(8,128)(2,1)S(1)} collective-permute-done((bf16[96,2048]{1,0:T(8,128)(2,1)S(1)}, bf16[96,2048]{1,0:T(8,128)(2,1)S(1)}, u32[]{:S(2)}, u32[]{:S(2)}) %collective-permute-start.13) | collective-permute-done | bytes 393248 | tf_op jit(solution)/shard_map/ppermute | solution.py:159
  165.0 39.6 %collective-permute-done.1 = bf16[144,2048]{1,0:T(8,128)(2,1)} collective-permute-done((bf16[144,2048]{1,0:T(8,128)(2,1)}, bf16[144,2048]{1,0:T(8,128)(2,1)}, u32[]{:S(2)}, u32[]{:S(2)}) %collective-permute-start.1) | collective-permute-done | bytes 589856 | tf_op jit(solution)/shard_map/ppermute | solution.py:170
  208.1 6.0 %collective-permute-start.29 = (bf16[256,2048]{1,0:T(8,128)(2,1)}, bf16[256,2048]{1,0:T(8,128)(2,1)}, u32[]{:S(2)}, u32[]{:S(2)}) collective-permute-start(bf16[256,2048]{1,0:T(8,128)(2,1)} %collective-permute-done.27.refs_9_), channel_id=1, source_target_pairs={{0,8},{4,12},{8,0},{12,4},{16,24},{20,28},{24,16},{28,20},{1,9},{5... | collective-permute-start | bytes 3145736 | tf_op jit(solution)/shard_map/ppermute | solution.py:159
  214.1 2.6 collective-permute-start.32
  221.0 16.8 %collective-permute-done.29.refs_11_ = bf16[256,2048]{1,0:T(8,128)(2,1)} collective-permute-done((bf16[256,2048]{1,0:T(8,128)(2,1)}, bf16[256,2048]{1,0:T(8,128)(2,1)}, u32[]{:S(2)}, u32[]{:S(2)}) %collective-permute-start.29) | collective-permute-done | bytes 1048608 | tf_op jit(solution)/shard_map/ppermute | solution.py:159
  240.1 22.4 %finish.1 = f32[8,512]{1,0:T(8,128)} custom-call(s32[1]{0:T(128)} %bitcast.flip_ref, s32[2,512,1]{2,1,0:T(8,128)} %copy.88.place_ref, f32[2,1,2048]{2,1,0:T(1,128)} %broadcast_in_dim.59.gain_ref, bf16[128,2048]{1,0:T(8,128)(2,1)} %copy-done.2, bf16[128,2048]{1,0:T(8,128)(2,1)} %slice.154.refs_1_, bf16[128,2048]{1,0:T(8,128)(2,1)} %collective-permute-done.2.refs_2_, ...), custom_call_target="tpu_custom_call" | custom-call | tf_op jit(solution)/shard_map/finish/pallas_call | solution.py:108
  262.5 5.4 %all-gather = f32[32,512]{1,0:T(8,128)S(1)} all-gather(f32[8,512]{1,0:T(8,128)} %finish.1), channel_id=2, replica_groups=mesh['expert'=8,'vocab'=4] {'vocab'}, dimensions={0}, use_global_device_ids=true | all-gather | bytes 81920 | tf_op jit(solution)/shard_map/all_gather | solution.py:294
  268.9 10.4 %all_to_all.5 = f32[8,5,2,128]{3,2,1,0:T(2,128)S(1)} all-to-all(f32[8,5,2,128]{3,2,1,0:T(2,128)S(1)} %constant_dynamic-update-slice_fusion.5), channel_id=1, replica_groups=mesh['expert'=8,'vocab'=4] {'expert'}, dimensions={0} | all-to-all | bytes 81920 | tf_op jit(solution)/shard_map/all_to_all | solution.py:303
  (163 shorter events, 43.7 us)
Async XLA Ops:
  2.6 26.7 %collective-permute-start.15 = (bf16[48,2048]{1,0:T(8,128)(2,1)S(1)}, bf16[48,2048]{1,0:T(8,128)(2,1)S(1)}, u32[]{:S(2)}, u32[]{:S(2)}) collective-permute-start(bf16[48,2048]{1,0:T(8,128)(2,1)S(1)} %get-tuple-element.21), channel_id=1, source_target_pairs={{0,16},{4,20},{8,24},{12,28},{16,0},{20,4},{24,8},{28,12},{1,17},{... | collective-permute-start | bytes 589832 | tf_op jit(solution)/shard_map/ppermute | solution.py:159
  6.7 28.1 %collective-permute-start.16 = (bf16[48,2048]{1,0:T(8,128)(2,1)S(1)}, bf16[48,2048]{1,0:T(8,128)(2,1)S(1)}, u32[]{:S(2)}, u32[]{:S(2)}) collective-permute-start(bf16[48,2048]{1,0:T(8,128)(2,1)S(1)} %get-tuple-element.24), channel_id=1, source_target_pairs={{0,20},{4,16},{8,28},{12,24},{16,4},{20,0},{24,12},{28,8},{1,21},{... | collective-permute-start | bytes 589832 | tf_op jit(solution)/shard_map/ppermute | solution.py:159
  8.0 26.8 %collective-permute-start.17 = (bf16[48,2048]{1,0:T(8,128)(2,1)S(1)}, bf16[48,2048]{1,0:T(8,128)(2,1)S(1)}, u32[]{:S(2)}, u32[]{:S(2)}) collective-permute-start(bf16[48,2048]{1,0:T(8,128)(2,1)S(1)} %get-tuple-element.23), channel_id=1, source_target_pairs={{0,24},{4,28},{8,16},{12,20},{16,8},{20,12},{24,0},{28,4},{1,25},{... | collective-permute-start | bytes 589832 | tf_op jit(solution)/shard_map/ppermute | solution.py:159
  11.6 23.2 %collective-permute-start.18 = (bf16[48,2048]{1,0:T(8,128)(2,1)S(1)}, bf16[48,2048]{1,0:T(8,128)(2,1)S(1)}, u32[]{:S(2)}, u32[]{:S(2)}) collective-permute-start(bf16[48,2048]{1,0:T(8,128)(2,1)S(1)} %get-tuple-element.22), channel_id=1, source_target_pairs={{0,28},{4,24},{8,20},{12,16},{16,12},{20,8},{24,4},{28,0},{1,29},{... | collective-permute-start | bytes 589832 | tf_op jit(solution)/shard_map/ppermute | solution.py:159
  34.9 19.9 %collective-permute-start.19 = (bf16[192,2048]{1,0:T(8,128)(2,1)S(1)}, bf16[192,2048]{1,0:T(8,128)(2,1)}, u32[]{:S(2)}, u32[]{:S(2)}) collective-permute-start(bf16[192,2048]{1,0:T(8,128)(2,1)S(1)} %bitcast.181), channel_id=1, source_target_pairs={{0,1},{1,0},{2,3},{3,2},{4,5},{5,4},{6,7},{7,6},{8,9},{9,8},{10,11... | collective-permute-start | bytes 2359304 | tf_op jit(solution)/shard_map/ppermute | solution.py:162
  54.8 14.3 %collective-permute-start.7 = (bf16[192,2048]{1,0:T(8,128)(2,1)}, bf16[192,2048]{1,0:T(8,128)(2,1)}, u32[]{:S(2)}, u32[]{:S(2)}) collective-permute-start(bf16[192,2048]{1,0:T(8,128)(2,1)} %bitcast.18), channel_id=1, source_target_pairs={{0,1},{1,0},{2,3},{3,2},{4,5},{5,4},{6,7},{7,6},{8,9},{9,8},{10,11... | collective-permute-start | bytes 2359304 | tf_op jit(solution)/shard_map/ppermute | solution.py:162
  68.6 17.4 %collective-permute-start.20 = (bf16[2,2,48,2048]{3,2,1,0:T(8,128)(2,1)}, bf16[2,2,48,2048]{3,2,1,0:T(8,128)(2,1)}, u32[]{:S(2)}, u32[]{:S(2)}) collective-permute-start(bf16[2,2,48,2048]{3,2,1,0:T(8,128)(2,1)} %dynamic-slice_bitcast_fusion), channel_id=1, source_target_pairs={{0,1},{1,0},{2,3},{3,2},{4,5},{5,4},{6,7},{7,6},{8,9},{9,8},{10,11... | collective-permute-start | bytes 2359304 | tf_op jit(solution)/shard_map/ppermute | solution.py:162
  84.3 54.7 %collective-permute-start = (bf16[144,2048]{1,0:T(8,128)(2,1)}, bf16[144,2048]{1,0:T(8,128)(2,1)S(1)}, u32[]{:S(2)}, u32[]{:S(2)}) collective-permute-start(bf16[144,2048]{1,0:T(8,128)(2,1)} %pad_maximum_fusion.4), channel_id=1, source_target_pairs={{0,0},{1,1},{2,4},{3,5},{4,2},{5,3},{6,6},{7,7},{8,8},{9,9},{10,12... | collective-permute-start | bytes 1769480 | tf_op jit(solution)/shard_map/ppermute | solution.py:170
  87.7 23.5 %collective-permute-start.21 = (bf16[2,48,2048]{2,1,0:T(8,128)(2,1)S(1)}, bf16[2,48,2048]{2,1,0:T(8,128)(2,1)S(1)}, u32[]{:S(2)}, u32[]{:S(2)}) collective-permute-start(bf16[2,48,2048]{2,1,0:T(8,128)(2,1)S(1)} %fusion.51), channel_id=1, source_target_pairs={{0,2},{1,3},{2,0},{3,1},{4,6},{5,7},{6,4},{7,5},{8,10},{9,11},{10,... | collective-permute-start | bytes 1179656 | tf_op jit(solution)/shard_map/ppermute | solution.py:162
  91.6 27.2 %collective-permute-start.9 = (bf16[2,48,2048]{2,1,0:T(8,128)(2,1)S(1)}, bf16[2,48,2048]{2,1,0:T(8,128)(2,1)S(1)}, u32[]{:S(2)}, u32[]{:S(2)}) collective-permute-start(bf16[2,48,2048]{2,1,0:T(8,128)(2,1)S(1)} %fusion.50), channel_id=1, source_target_pairs={{0,2},{1,3},{2,0},{3,1},{4,6},{5,7},{6,4},{7,5},{8,10},{9,11},{10,... | collective-permute-start | bytes 1179656 | tf_op jit(solution)/shard_map/ppermute | solution.py:162
  112.7 24.3 %collective-permute-start.23 = (bf16[96,2048]{1,0:T(8,128)(2,1)S(1)}, bf16[96,2048]{1,0:T(8,128)(2,1)}, u32[]{:S(2)}, u32[]{:S(2)}) collective-permute-start(bf16[96,2048]{1,0:T(8,128)(2,1)S(1)} %bitcast.192), channel_id=1, source_target_pairs={{0,16},{1,24},{2,18},{3,26},{4,20},{5,28},{6,22},{7,30},{8,17},{9,... | collective-permute-start | bytes 1179656 | tf_op jit(solution)/shard_map/ppermute | solution.py:170
  118.9 18.5 %collective-permute-start.10 = (bf16[96,2048]{1,0:T(8,128)(2,1)S(1)}, bf16[96,2048]{1,0:T(8,128)(2,1)S(1)}, u32[]{:S(2)}, u32[]{:S(2)}) collective-permute-start(bf16[96,2048]{1,0:T(8,128)(2,1)S(1)} %bitcast.189), channel_id=1, source_target_pairs={{0,0},{1,8},{2,2},{3,10},{4,4},{5,12},{6,6},{7,14},{8,1},{9,9},{10... | collective-permute-start | bytes 1179656 | tf_op jit(solution)/shard_map/ppermute | solution.py:170
  119.8 29.8 %collective-permute-start.11 = (bf16[96,2048]{1,0:T(8,128)(2,1)S(1)}, bf16[96,2048]{1,0:T(8,128)(2,1)S(1)}, u32[]{:S(2)}, u32[]{:S(2)}) collective-permute-start(bf16[96,2048]{1,0:T(8,128)(2,1)S(1)} %bitcast.190), channel_id=1, source_target_pairs={{0,16},{1,24},{2,18},{3,26},{4,20},{5,28},{6,22},{7,30},{8,17},{9,... | collective-permute-start | bytes 1179656 | tf_op jit(solution)/shard_map/ppermute | solution.py:170
  123.4 26.5 %collective-permute-start.24 = (bf16[96,2048]{1,0:T(8,128)(2,1)}, bf16[96,2048]{1,0:T(8,128)(2,1)S(1)}, u32[]{:S(2)}, u32[]{:S(2)}) collective-permute-start(bf16[96,2048]{1,0:T(8,128)(2,1)} %collective-permute-done.22), channel_id=1, source_target_pairs={{0,4},{4,0},{8,12},{12,8},{16,20},{20,16},{24,28},{28,24},{1,5},{5... | collective-permute-start | bytes 1179656 | tf_op jit(solution)/shard_map/ppermute | solution.py:159
  137.4 19.3 %collective-permute-start.12 = (bf16[96,2048]{1,0:T(8,128)(2,1)S(1)}, bf16[96,2048]{1,0:T(8,128)(2,1)S(1)}, u32[]{:S(2)}, u32[]{:S(2)}) collective-permute-start(bf16[96,2048]{1,0:T(8,128)(2,1)S(1)} %collective-permute-done.10), channel_id=1, source_target_pairs={{0,4},{4,0},{8,12},{12,8},{16,20},{20,16},{24,28},{28,24},{1,5},{5... | collective-permute-start | bytes 1179656 | tf_op jit(solution)/shard_map/ppermute | solution.py:159
  139.0 65.6 %collective-permute-start.27 = (bf16[256,2048]{1,0:T(8,128)(2,1)}, bf16[256,2048]{1,0:T(8,128)(2,1)}, u32[]{:S(2)}, u32[]{:S(2)}) collective-permute-start(bf16[256,2048]{1,0:T(8,128)(2,1)} %refs_8_.1), channel_id=1, source_target_pairs={{0,2},{1,3},{2,0},{3,1},{4,6},{5,7},{6,4},{7,5},{8,10},{9,11},{10,... | collective-permute-start | bytes 3145736 | tf_op jit(solution)/shard_map/ppermute | solution.py:162
  149.9 58.0 %collective-permute-start.31 = (bf16[256,2048]{1,0:T(8,128)(2,1)}, bf16[256,2048]{1,0:T(8,128)(2,1)}, u32[]{:S(2)}, u32[]{:S(2)}) collective-permute-start(bf16[256,2048]{1,0:T(8,128)(2,1)} %refs_12_.1), channel_id=1, source_target_pairs={{0,8},{4,12},{8,0},{12,4},{16,24},{20,28},{24,16},{28,20},{1,9},{5... | collective-permute-start | bytes 3145736 | tf_op jit(solution)/shard_map/ppermute | solution.py:159
  150.5 57.6 %collective-permute-start.28 = (bf16[256,2048]{1,0:T(8,128)(2,1)}, bf16[256,2048]{1,0:T(8,128)(2,1)}, u32[]{:S(2)}, u32[]{:S(2)}) collective-permute-start(bf16[256,2048]{1,0:T(8,128)(2,1)} %refs_8_.1), channel_id=1, source_target_pairs={{0,8},{4,12},{8,0},{12,4},{16,24},{20,28},{24,16},{28,20},{1,9},{5... | collective-permute-start | bytes 3145736 | tf_op jit(solution)/shard_map/ppermute | solution.py:159
  156.7 57.4 %collective-permute-start.30 = (bf16[256,2048]{1,0:T(8,128)(2,1)}, bf16[256,2048]{1,0:T(8,128)(2,1)}, u32[]{:S(2)}, u32[]{:S(2)}) collective-permute-start(bf16[256,2048]{1,0:T(8,128)(2,1)} %refs_12_.1), channel_id=1, source_target_pairs={{0,2},{1,3},{2,0},{3,1},{4,6},{5,7},{6,4},{7,5},{8,10},{9,11},{10,... | collective-permute-start | bytes 3145736 | tf_op jit(solution)/shard_map/ppermute | solution.py:162
  160.9 43.7 %collective-permute-start.1 = (bf16[144,2048]{1,0:T(8,128)(2,1)}, bf16[144,2048]{1,0:T(8,128)(2,1)}, u32[]{:S(2)}, u32[]{:S(2)}) collective-permute-start(bf16[144,2048]{1,0:T(8,128)(2,1)} %pad_maximum_fusion.4), channel_id=1, source_target_pairs={{0,16},{1,17},{2,20},{3,21},{4,18},{5,19},{6,22},{7,23},{8,24},{9,... | collective-permute-start | bytes 1769480 | tf_op jit(solution)/shard_map/ppermute | solution.py:170
  204.7 35.4 %collective-permute-start.26 = (bf16[2,192,2048]{2,1,0:T(8,128)(2,1)S(1)}, bf16[2,192,2048]{2,1,0:T(8,128)(2,1)}, u32[]{:S(2)}, u32[]{:S(2)}) collective-permute-start(bf16[2,192,2048]{2,1,0:T(8,128)(2,1)S(1)} %bitcast.175), channel_id=1, source_target_pairs={{0,1},{1,0},{2,3},{3,2},{4,5},{5,4},{6,7},{7,6},{8,9},{9,8},{10,11... | collective-permute-start | bytes 4718600 | tf_op jit(solution)/shard_map/ppermute | solution.py:162
  204.7 35.4 %collective-permute-start.14 = (bf16[2,192,2048]{2,1,0:T(8,128)(2,1)}, bf16[2,192,2048]{2,1,0:T(8,128)(2,1)}, u32[]{:S(2)}, u32[]{:S(2)}) collective-permute-start(bf16[2,192,2048]{2,1,0:T(8,128)(2,1)} %bitcast.31.refs_4_), channel_id=1, source_target_pairs={{0,1},{1,0},{2,3},{3,2},{4,5},{5,4},{6,7},{7,6},{8,9},{9,8},{10,11... | collective-permute-start | bytes 4718600 | tf_op jit(solution)/shard_map/ppermute | solution.py:162
  208.1 29.7 %collective-permute-start.29 = (bf16[256,2048]{1,0:T(8,128)(2,1)}, bf16[256,2048]{1,0:T(8,128)(2,1)}, u32[]{:S(2)}, u32[]{:S(2)}) collective-permute-start(bf16[256,2048]{1,0:T(8,128)(2,1)} %collective-permute-done.27.refs_9_), channel_id=1, source_target_pairs={{0,8},{4,12},{8,0},{12,4},{16,24},{20,28},{24,16},{28,20},{1,9},{5... | collective-permute-start | bytes 3145736 | tf_op jit(solution)/shard_map/ppermute | solution.py:159
  214.1 26.0 %collective-permute-start.32 = (bf16[256,2048]{1,0:T(8,128)(2,1)}, bf16[256,2048]{1,0:T(8,128)(2,1)}, u32[]{:S(2)}, u32[]{:S(2)}) collective-permute-start(bf16[256,2048]{1,0:T(8,128)(2,1)} %collective-permute-done.31.refs_14_), channel_id=1, source_target_pairs={{0,2},{1,3},{2,0},{3,1},{4,6},{5,7},{6,4},{7,5},{8,10},{9,11},{10,... | collective-permute-start | bytes 3145736 | tf_op jit(solution)/shard_map/ppermute | solution.py:162
  (27 other events, 389.9 us)
where the time goes:
time: 280 us
  waiting for transfers between devices  143 us (51%)
  starting transfers between devices  51.3 us (18%)
  matrix products  26.2 us (9%)
  Pallas kernels  22.4 us (8%)
  blocking collectives  15.8 us (6%)
  other arithmetic  11.6 us (4%)
  local copies, waits for them, and re-layouts  8.97 us (3%)
    ppermute x6, waiting for transfers between devices, by_both(): return lax.ppermute(array, BOTH, perm)  61.6 us
    ppermute x14, waiting for transfers between devices, by_expert(): return lax.ppermute(array, 'expert', [(s, move(s)) for s in range(En)])  56 us
    ppermute x14, starting transfers between devices, by_expert(): return lax.ppermute(array, 'expert', [(s, move(s)) for s in range(En)])  30.6 us
    dot_general x2, matrix products, ffn(): jnp.dot(hidden, weight_out, preferred_element_type=jnp.float32)  25.7 us
    ppermute x13, waiting for transfers between devices, by_vocab(): return lax.ppermute(array, 'vocab', [(s, move(s)) for s in range(Vn)])  25.4 us
    pallas_call x1, Pallas kernels, finish(): pl.pallas_call(kernel, in_specs=[pl.BlockSpec(memory_space=pltpu.SMEM), p...  22.4 us
    ppermute x6, starting transfers between devices, by_both(): return lax.ppermute(array, BOTH, perm)  11.4 us
    all_to_all x1, blocking collectives, local(): lax.all_to_all(jnp.stack(letters), 'expert', split_axis=0, concat_axis=0,...  10.4 us
  transfers between devices with their start and end apart: 33, of which 14 were waited for; matrix products, arithmetic and copies ran while one was open for 15% of the time, Pallas kernels for 0%

commit v1 on v0

v1 whole, which is shorter than its diff:
```python
import jax
import jax.numpy as jnp
from jax import lax
from jax.experimental import pallas as pl
from jax.experimental.pallas import tpu as pltpu
from jax.sharding import PartitionSpec as P


BOTH = ("expert", "vocab")

LIFT = 2.0**60
LIMIT = 8.0


def seats(expert, ranking, cap, kinds):
    numbers = jnp.arange(expert.shape[0], dtype=jnp.int32)
    same_expert = expert[:, None] == expert[None, :]
    before = ranking[None, :] < ranking[:, None]
    rank = jnp.sum(jnp.logical_and(same_expert, before).astype(jnp.int32), axis=1)
    kept = rank < cap
    earlier = jnp.logical_and(numbers[None, :] < numbers[:, None], jnp.logical_not(kept)[None, :])
    turn = jnp.sum(earlier.astype(jnp.int32), axis=1)
    kind = jnp.arange(kinds, dtype=jnp.int32)
    used = jnp.sum((expert[None, :] == kind[:, None]).astype(jnp.int32), axis=1)
    used = jnp.minimum(used, cap)
    start = jnp.sum(jnp.where(kind[None, :] < kind[:, None], cap - used[None, :], 0), axis=1)
    stop = start + cap - used
    fits = jnp.logical_and(turn[None, :] >= start[:, None], turn[None, :] < stop[:, None])
    spare = jnp.sum(jnp.where(fits, kind[:, None], 0), axis=0)
    slot = jnp.sum(jnp.where(fits, (used - start)[:, None] + turn[None, :], 0), axis=0)
    return jnp.where(kept, expert, spare), jnp.where(kept, rank, slot), kept


def ffn(rows, weight_in, weight_out):
    hidden = jax.nn.gelu(
        jnp.dot(rows, weight_in, preferred_element_type=jnp.float32)
    ).astype(jnp.bfloat16)
    return jnp.dot(hidden, weight_out, preferred_element_type=jnp.float32).astype(jnp.bfloat16)


def set_of(w):
    return (w & 1) | ((w >> 2) << 1), (w >> 1) & 1


def finish(where, gains, numbers, pools, t_shards, s_shards, count):
    width = gains.shape[-1]
    J = len(numbers)
    H = len(pools) // (2 * J)
    lanes = -(-count // 128) * 128
    rows = count * J
    tile = min(rows, 256)
    height = pools[0][0].shape[0]
    half = height // 2
    reach = height * len(pools)
    entries = t_shards[0].shape[0]
    span = entries * len(t_shards)
    shards = list(t_shards) + list(s_shards)
    counts = (J, len(pools), len(shards))

    def kernel(where_ref, gain_in, *refs):
        y, c, me, zh, zl = [where_ref[i] for i in range(5)]
        number_in, refs = refs[:J], refs[J:]
        pool_in, refs = refs[: 2 * counts[1]], refs[2 * counts[1] :]
        head_in, refs = refs[: counts[2]], refs[counts[2] :]
        out_ref, number, place, gain_ref, pool, head, normed, logits = refs[:8]
        small_sem, pool_sem, head_sem = refs[8:]
        copies = {}

        def begin(name, source, target, sem):
            copies[name] = pltpu.make_async_copy(source, target, sem)
            copies[name].start()

        def pool_copy(branch, i, kind):
            return pltpu.make_async_copy(
                pool_in[2 * i + kind],
                pool.at[branch, pl.ds(i * height, height)],
                pool_sem.at[branch, i],
            )

        def begin_pool(branch):
            for i in range(counts[1]):
                for kind in range(2):

                    @pl.when(y ^ branch == kind)
                    def _():
                        pool_copy(branch, i, kind).start()

        def begin_heads(branch):
            for i in range(counts[2] // 2):
                n = branch * (counts[2] // 2) + i
                begin(
                    ("head", n),
                    head_in[n],
                    head.at[branch, pl.ds(i * entries, entries)],
                    head_sem.at[n],
                )

        for i in range(J):
            begin(("number", i), number_in[i], number.at[i], small_sem.at[i])
        begin_pool(0)
        begin("gain", gain_in, gain_ref, small_sem.at[J])
        for i in range(J):
            copies["number", i].wait()
            values = number[i].astype(jnp.float32).astype(jnp.int32)
            table = []
            for branch in range(2):
                phase, side, round_, upper, low = [
                    values[5 * branch + n : 5 * branch + n + 1] for n in range(5)
                ]
                row = ((phase ^ me ^ i) * 2 + (side ^ c)) * H + (round_ ^ zh)
                row = row * height + (upper ^ zl) * half + low
                table.append(row.astype(jnp.float32))
            table.append(jnp.zeros((6, lanes), jnp.float32))
            column = jnp.concatenate(table, axis=0).T
            place[i * count : (i + 1) * count] = column[:count]
        for branch in range(2):
            for i in range(counts[1]):
                pool_copy(branch, i, 0).wait()
            if branch == 0:
                copies["gain"].wait()
                begin_pool(1)
            begin_heads(branch)
            for t in range(rows // tile):
                here = pl.ds(t * tile, tile)
                columns = lax.broadcasted_iota(jnp.int32, (tile, reach), 1).astype(jnp.float32)
                picked = jnp.where(columns == place[here, branch : branch + 1], 1.0, 0.0)
                total = jnp.dot(
                    picked.astype(jnp.bfloat16), pool[branch], preferred_element_type=jnp.float32
                )
                mean = jnp.mean(total * total, axis=-1, keepdims=True)
                scaled = total * lax.rsqrt(mean + 1e-05) * gain_ref[branch]
                normed[branch, here, :] = scaled.astype(jnp.bfloat16)
        for branch in range(2):
            for i in range(counts[2] // 2):
                copies["head", branch * (counts[2] // 2) + i].wait()
            for t in range(rows // 512):
                logits[branch, :, t*512:(t+1)*512] = lax.dot_general(
                    head[branch], normed[branch, t*512:(t+1)*512, :],
                    (((1,), (1,)), ((), ())),
                    preferred_element_type=jnp.float32,
                )
        for t in range(rows // 128):
            here = slice(t * 128, (t + 1) * 128)
            teacher, student = logits[0, :, here], logits[1, :, here]
            tp = jnp.max(teacher, axis=0, keepdims=True)
            sp = jnp.max(student, axis=0, keepdims=True)
            te = jnp.exp(teacher - tp)
            table = [
                tp,
                jnp.sum(te, axis=0, keepdims=True),
                jnp.sum(te * (teacher - student), axis=0, keepdims=True),
                sp,
                jnp.sum(jnp.exp(student - sp), axis=0, keepdims=True),
            ]
            out_ref[:, here] = jnp.concatenate(table + [jnp.zeros((3, 128), jnp.float32)], axis=0)

    return pl.pallas_call(
        kernel,
        in_specs=[
            pl.BlockSpec(memory_space=pltpu.SMEM),
        ]
        + [pl.BlockSpec(memory_space=pl.ANY)] * (sum(counts) + counts[1] + 1),
        out_specs=pl.BlockSpec(memory_space=pltpu.VMEM),
        out_shape=jax.ShapeDtypeStruct((8, rows), jnp.float32),
        scratch_shapes=[
            pltpu.VMEM((J, 16, lanes), jnp.bfloat16),
            pltpu.VMEM((rows, 8), jnp.float32),
            pltpu.VMEM(gains.shape, gains.dtype),
            pltpu.VMEM((2, reach, width), jnp.bfloat16),
            pltpu.VMEM((2, span, width), jnp.bfloat16),
            pltpu.VMEM((2, rows, width), jnp.bfloat16),
            pltpu.VMEM((2, span, rows), jnp.float32),
            pltpu.SemaphoreType.DMA((J + 1,)),
            pltpu.SemaphoreType.DMA((2, counts[1])),
            pltpu.SemaphoreType.DMA((counts[2],)),
        ],
        name="finish",
    )(where, gains, *numbers, *[a for pair in pools for a in pair], *shards)


def local(
    tokens,
    teacher_expert,
    student_expert,
    priority,
    expert_in,
    expert_out,
    teacher_gain,
    student_gain,
    teacher_head,
    student_head,
):
    count, width = tokens.shape
    En = lax.axis_size("expert")
    Vn = lax.axis_size("vocab")
    J = En // Vn
    H = En // 4
    X = Vn // 2
    cap = 3 * count // En
    hc = cap // 2
    e = lax.axis_index("expert")
    v = lax.axis_index("vocab")
    x, c = v // 2, v % 2
    zh, zl, y = e // 4, (e // 2) % 2, e % 2

    def by_expert(array, move):
        return lax.ppermute(array, "expert", [(s, move(s)) for s in range(En)])

    def by_vocab(array, move):
        perm = [(s, move(s)) for s in range(Vn)]
        return lax.ppermute(array, "vocab", [pair for pair in perm if pair[1] is not None])

    def by_both(array, move):
        perm = []
        for s in range(En):
            for u in range(Vn):
                target = move(s, u)
                if target is not None:
                    perm.append((s * Vn + u, target[0] * Vn + target[1]))
        return lax.ppermute(array, BOTH, perm)

    other_core = lambda array: by_vocab(array, lambda u: u ^ 1)

    ranking = priority[0]
    lifted = jnp.max(jnp.abs(tokens), axis=1).astype(jnp.float32) * LIFT
    lifted = jnp.where(lifted > LIMIT, LIFT, 0.0)
    group_rows = jnp.arange(En * hc, dtype=jnp.int32)[:, None]
    chosen = jnp.zeros((En * hc, count), jnp.float32)
    numbers = []
    for lane, expert in enumerate((teacher_expert[:, 0], student_expert[:, 0])):
        expert, slot, kept = seats(expert, ranking, cap, En // 2)
        source = 2 * expert + lane
        numbers += [source // Vn, source // 2 % 2, source // 4, slot // hc, slot % hc]
        place = jnp.where(slot // hc == c, (source ^ e) * hc + slot % hc, -1)
        weight = jnp.where(kept, 1.0, lifted)
        chosen = jnp.where(group_rows == place[None, :], weight[None, :], chosen)
    outgoing = jnp.dot(chosen.astype(jnp.bfloat16), tokens, preferred_element_type=jnp.float32)
    outgoing = outgoing.astype(jnp.bfloat16).reshape(En, hc, width)

    order = [m1 * 2 + (xi & 1) + ((xi >> 1) << 2) for m1 in range(2) for xi in range(X)]
    arrived = {0: outgoing[0]}
    for g in range(1, En):
        arrived[g] = by_expert(outgoing[g], lambda s: s ^ g)

    t_shards, s_shards = [teacher_head], [student_head]
    for d in range(1, X):
        t_shards.append(by_vocab(teacher_head, lambda u: u ^ (2 * d)))
        s_shards.append(by_vocab(student_head, lambda u: u ^ (2 * d)))
    s_far = by_expert(student_head, lambda s: s ^ 2)
    t_far = by_expert(teacher_head, lambda s: s ^ 2)
    t_diag = [by_expert(t_shards[d], lambda s: s ^ 2) for d in range(1, X)]
    s_diag = [by_vocab(s_far, lambda u: u ^ (2 * d)) for d in range(1, X)]
    t_shards += [t_far] + t_diag
    s_shards += [s_far] + s_diag

    def set_route(rho):
        def move(s, u):
            q = ((s // Vn) ^ rho) * Vn + u
            xd, zld = set_of(s % Vn)
            return (q >> 2) * 4 + zld * 2 + ((q >> 1) & 1), 2 * xd + (q & 1)

        return move

    numbers = jnp.stack(numbers).astype(jnp.bfloat16)
    numbers = jnp.pad(numbers, ((0, 16 - numbers.shape[0]), (0, -count % 128)))
    set_numbers = [by_both(numbers, set_route(rho)) for rho in range(J)]

    weight_in = expert_in[0]
    weight_out = expert_out[0]
    xe, _ = set_of(e % Vn)
    pools = []
    for r in range(J):
        own = jnp.stack([arrived[r * Vn + m] for m in order]).reshape(Vn * hc, width)
        rows = jnp.concatenate([own, other_core(own)], axis=0)
        partial = ffn(rows, weight_in, weight_out).reshape(2, 2, X, hc, width)
        kept_side = zl ^ c
        sent = lax.dynamic_index_in_dim(partial, 1 - kept_side, 1, keepdims=False)
        kept = lax.dynamic_index_in_dim(partial, kept_side, 1, keepdims=False)
        got = other_core(sent)
        summed = kept.astype(jnp.float32) + got[::-1].astype(jnp.float32)
        total = lax.dynamic_index_in_dim(summed, xe ^ x, 1, keepdims=False)
        narrow = summed.astype(jnp.bfloat16)
        for d in range(1, X):
            part = lax.dynamic_index_in_dim(narrow, xe ^ x ^ d, 1, keepdims=False)
            part = by_vocab(part, lambda u: u ^ (2 * d))
            total = total + part.astype(jnp.float32)
        own = lax.dynamic_index_in_dim(
            rows.reshape(2, 2, X, hc, width), kept_side, 1, keepdims=False
        )
        own = lax.dynamic_index_in_dim(own, xe ^ x, 1, keepdims=False).astype(jnp.float32)
        passing = jnp.max(jnp.abs(own), axis=-1, keepdims=True) > LIMIT
        total = jnp.where(passing, own * (1.0 / LIFT), own + total)
        reduced = total.astype(jnp.bfloat16).reshape(cap, width)
        mine, crossed = [], []
        for q in range(H):

            def spread(s, u):
                return ((s // 4) ^ q) * 4 + (u % 2) * 2 + s % 2, (u // 2) * 2 + (s // 2) % 2

            mine.append(by_both(reduced, spread))
            crossed.append(by_expert(mine[-1], lambda s: s ^ 1))
        pools += list(zip(mine, crossed))
        theirs = [other_core(mine[q]) for q in range(H)]
        far = [other_core(crossed[q]) for q in range(H)]
        pools += list(zip(theirs, far))

    me = ((zh * 2 + y) * 2 + c) // Vn
    stats = finish(
        jnp.stack([y, c, me, zh, zl]).astype(jnp.int32),
        jnp.stack([teacher_gain, student_gain])[:, None, :],
        set_numbers,
        pools,
        t_shards,
        s_shards,
        count,
    )

    def merge(parts, axis):
        tp, tt, tw, sp, st = [lax.index_in_dim(parts, i, axis + 1, keepdims=False) for i in range(5)]
        tpm = jnp.max(tp, axis=axis, keepdims=True)
        spm = jnp.max(sp, axis=axis, keepdims=True)
        tr, sr = jnp.exp(tp - tpm), jnp.exp(sp - spm)
        return (
            jnp.squeeze(tpm, axis),
            jnp.sum(tt * tr, axis=axis),
            jnp.sum(tw * tr, axis=axis),
            jnp.squeeze(spm, axis),
            jnp.sum(st * sr, axis=axis),
        )

    everyone = lax.all_gather(stats, "vocab", axis=0).reshape(X, 2, 8, J, count)
    by_x = jnp.stack(merge(everyone, 1), axis=1)
    neutral = jnp.array([-1e30, 0.0, 0.0, -1e30, 0.0], jnp.float32)[:, None]
    letters = []
    for b in range(En):
        xb, zb = set_of(b % Vn)
        letter = lax.dynamic_index_in_dim(by_x[xb], me ^ (b // Vn), 1, keepdims=False)
        letters.append(jnp.where(zl == zb, letter, neutral))
    mail = lax.all_to_all(jnp.stack(letters), "expert", split_axis=0, concat_axis=0, tiled=True)
    tp, tt, tw, sp, st = merge(mail, 0)
    return tw / tt - tp - jnp.log(tt) + sp + jnp.log(st)


def solution(mesh):
    in_specs = (
        P("expert", None),
        P("expert", None),
        P("expert", None),
        P("expert", None),
        P("expert", None, "vocab"),
        P("expert", "vocab", None),
        P(),
        P(),
        P(("vocab", "expert"), None),
        P(("vocab", "expert"), None),
    )
    out_specs = P("expert")

    return jax.shard_map(local, mesh=mesh, in_specs=in_specs, out_specs=out_specs, check_vma=False)
```

time: 280 us -> 245 us (0.88)
  waiting for transfers between devices: 143 us -> 116 us
  Pallas kernels: 22.4 us -> 13.4 us
  local copies, waits for them, and re-layouts: 8.97 us -> 3.52 us
    ppermute x6, waiting for transfers between devices: 61.6 us -> 31.8 us  [by_both(): return lax.ppermute(array, BOTH, perm)]
    ppermute x13 -> x17, waiting for transfers between devices: 25.4 us -> 49.1 us  [by_vocab(): lax.ppermute(array, 'vocab', [pair for pair in perm if pair[1] is not None])]
    ppermute x14, waiting for transfers between devices: 56 us -> 35 us  [by_expert(): return lax.ppermute(array, 'expert', [(s, move(s)) for s in range(En)])]
    pallas_call x1, Pallas kernels: 22.4 us -> 13.4 us  [finish(): pl.pallas_call(kernel, in_specs=[pl.BlockSpec(memory_space=pltpu.SMEM)] +...]
    ppermute x13 -> x17, starting transfers between devices: 9.24 us -> 14.5 us  [by_vocab(): lax.ppermute(array, 'vocab', [pair for pair in perm if pair[1] is not None])]
    slice x10 -> x1, local copies, waits for them, and re-layouts: 3.9 us -> 0.01 us  [local(): letter = lax.dynamic_index_in_dim(by_x[xb], me ^ b // Vn, 1, keepdims=False)]
    another operation x4 -> x3, other arithmetic: 3.17 us -> 0.07 us  [the longest x2 3.16 us: local(): mine = jnp.stack(mine + crossed).reshape(2, H * cap, width)]
    ppermute x6, starting transfers between devices: 11.4 us -> 8.61 us  [by_both(): return lax.ppermute(array, BOTH, perm)]
  transfers between devices with their start and end apart: 33 -> 37, of which waited for: 14 -> 10; matrix products, arithmetic and copies ran while one was open for 15% -> 14% of each run, Pallas kernels for 0% -> 0%
where the time goes in v1:
time: 245 us
  waiting for transfers between devices  116 us (47%)
  starting transfers between devices  53.3 us (22%)
  matrix products  27.4 us (11%)
  blocking collectives  18 us (7%)
  Pallas kernels  13.4 us (5%)
  other arithmetic  12.7 us (5%)
  local copies, waits for them, and re-layouts  3.52 us (1%)
    ppermute x17, waiting for transfers between devices, by_vocab(): lax.ppermute(array, 'vocab', [pair for pair in perm if pair[1] is not None])  49.1 us
    ppermute x14, waiting for transfers between devices, by_expert(): return lax.ppermute(array, 'expert', [(s, move(s)) for s in range(En)])  35 us
    ppermute x6, waiting for transfers between devices, by_both(): return lax.ppermute(array, BOTH, perm)  31.8 us
    ppermute x14, starting transfers between devices, by_expert(): return lax.ppermute(array, 'expert', [(s, move(s)) for s in range(En)])  30.2 us
    dot_general x2, matrix products, ffn(): jnp.dot(hidden, weight_out, preferred_element_type=jnp.float32)  25.6 us
    ppermute x17, starting transfers between devices, by_vocab(): lax.ppermute(array, 'vocab', [pair for pair in perm if pair[1] is not None])  14.5 us
    pallas_call x1, Pallas kernels, finish(): pl.pallas_call(kernel, in_specs=[pl.BlockSpec(memory_space=pltpu.SMEM)] +...  13.4 us
    all_to_all x1, blocking collectives, local(): lax.all_to_all(jnp.stack(letters), 'expert', split_axis=0, concat_axis=0,...  12.6 us
  transfers between devices with their start and end apart: 37, of which 10 were waited for; matrix products, arithmetic and copies ran while one was open for 14% of the time, Pallas kernels for 0%

profile of v1, /device:TPU:0, one launch (start us, length us, event | category | flops | bytes accessed | tf_op | source)
XLA Modules:
  0.0 244.9 jit_solution(13484920914629447563)
XLA Ops:
  5.6 1.8 convolution_convert_fusion
  7.6 4.1 %collective-permute-start.16 = (bf16[48,2048]{1,0:T(8,128)(2,1)S(1)}, bf16[48,2048]{1,0:T(8,128)(2,1)S(1)}, u32[]{:S(2)}, u32[]{:S(2)}) collective-permute-start(bf16[48,2048]{1,0:T(8,128)(2,1)S(1)} %get-tuple-element.23), channel_id=1, source_target_pairs={{0,16},{4,20},{8,24},{12,28},{16,0},{20,4},{24,8},{28,12},{1,17},{... | collective-permute-start | bytes 589832 | tf_op jit(solution)/shard_map/ppermute | solution.py:207
  13.0 3.6 %collective-permute-start.18 = (bf16[48,2048]{1,0:T(8,128)(2,1)S(1)}, bf16[48,2048]{1,0:T(8,128)(2,1)S(1)}, u32[]{:S(2)}, u32[]{:S(2)}) collective-permute-start(bf16[48,2048]{1,0:T(8,128)(2,1)S(1)} %get-tuple-element.25), channel_id=1, source_target_pairs={{0,24},{4,28},{8,16},{12,20},{16,8},{20,12},{24,0},{28,4},{1,25},{... | collective-permute-start | bytes 589832 | tf_op jit(solution)/shard_map/ppermute | solution.py:207
  16.6 1.7 collective-permute-start.2
  18.3 16.0 %collective-permute-done.16 = bf16[48,2048]{1,0:T(8,128)(2,1)S(1)} collective-permute-done((bf16[48,2048]{1,0:T(8,128)(2,1)S(1)}, bf16[48,2048]{1,0:T(8,128)(2,1)S(1)}, u32[]{:S(2)}, u32[]{:S(2)}) %collective-permute-start.16) | collective-permute-done | bytes 196640 | tf_op jit(solution)/shard_map/ppermute | solution.py:207
  34.3 5.5 %collective-permute-done.17 = bf16[48,2048]{1,0:T(8,128)(2,1)S(1)} collective-permute-done((bf16[48,2048]{1,0:T(8,128)(2,1)S(1)}, bf16[48,2048]{1,0:T(8,128)(2,1)S(1)}, u32[]{:S(2)}, u32[]{:S(2)}) %collective-permute-start.17) | collective-permute-done | bytes 196640 | tf_op jit(solution)/shard_map/ppermute | solution.py:207
  41.7 9.2 %collective-permute-start.32 = (bf16[256,2048]{1,0:T(8,128)(2,1)}, bf16[256,2048]{1,0:T(8,128)(2,1)}, u32[]{:S(2)}, u32[]{:S(2)}) collective-permute-start(bf16[256,2048]{1,0:T(8,128)(2,1)} %refs_18_.1), channel_id=1, source_target_pairs={{0,8},{4,12},{8,0},{12,4},{16,24},{20,28},{24,16},{28,20},{1,9},{5... | collective-permute-start | bytes 3145736 | tf_op jit(solution)/shard_map/ppermute | solution.py:207
  51.4 12.7 %fusion.27 = bf16[384,2048]{1,0:T(8,128)(2,1)S(1)} fusion(bf16[1,2048,2048]{2,1,0:T(8,128)(2,1)} %param.16, bf16[1,2048,2048]{2,1,0:T(8,128)(2,1)} %param.15, bf16[192,2048]{1,0:T(8,128)(2,1)} %collective-permute-done.20, bf16[192,2048]{1,0:T(8,128)(2,1)S(1)} %bitcast.196), kind=kOutput, calls=%fused_computation.27 | convolution fusion | flops 6453460992 | bytes 19922944 | tf_op jit(solution)/shard_map/dot_general | solution.py:38
  65.5 12.9 %fusion.24 = bf16[384,2048]{1,0:T(8,128)(2,1)S(1)} fusion(bf16[1,2048,2048]{2,1,0:T(8,128)(2,1)} %param.16, bf16[1,2048,2048]{2,1,0:T(8,128)(2,1)} %param.15, bf16[192,2048]{1,0:T(8,128)(2,1)} %collective-permute-done.5, bf16[192,2048]{1,0:T(8,128)(2,1)S(1)} %bitcast.199), kind=kOutput, calls=%fused_computation.26 | convolution fusion | flops 6453460992 | bytes 19922944 | tf_op jit(solution)/shard_map/dot_general | solution.py:38
  83.8 3.6 %collective-permute-start.1 = (bf16[16,256]{1,0:T(8,128)(2,1)S(1)}, bf16[16,256]{1,0:T(8,128)(2,1)S(1)}, u32[]{:S(2)}, u32[]{:S(2)}) collective-permute-start(bf16[16,256]{1,0:T(8,128)(2,1)S(1)} %pad.4), channel_id=1, source_target_pairs={{0,16},{1,17},{2,20},{3,21},{4,18},{5,19},{6,22},{7,23},{8,24},{9,... | collective-permute-start | bytes 24584 | tf_op jit(solution)/shard_map/ppermute | solution.py:220
  87.4 6.6 %collective-permute-start.22 = (bf16[2,48,2048]{2,1,0:T(8,128)(2,1)S(1)}, bf16[2,48,2048]{2,1,0:T(8,128)(2,1)S(1)}, u32[]{:S(2)}, u32[]{:S(2)}) collective-permute-start(bf16[2,48,2048]{2,1,0:T(8,128)(2,1)S(1)} %fusion.45), channel_id=1, source_target_pairs={{0,2},{1,3},{2,0},{3,1},{4,6},{5,7},{6,4},{7,5},{8,10},{9,11},{10,... | collective-permute-start | bytes 1179656 | tf_op jit(solution)/shard_map/ppermute | solution.py:211
  94.3 2.6 %collective-permute-done.1.refs_1_ = bf16[16,256]{1,0:T(8,128)(2,1)S(1)} collective-permute-done((bf16[16,256]{1,0:T(8,128)(2,1)S(1)}, bf16[16,256]{1,0:T(8,128)(2,1)S(1)}, u32[]{:S(2)}, u32[]{:S(2)}) %collective-permute-start.1) | collective-permute-done | bytes 8224 | tf_op jit(solution)/shard_map/ppermute | solution.py:220
  98.3 5.1 %collective-permute-start.33 = (bf16[256,2048]{1,0:T(8,128)(2,1)}, bf16[256,2048]{1,0:T(8,128)(2,1)S(1)}, u32[]{:S(2)}, u32[]{:S(2)}) collective-permute-start(bf16[256,2048]{1,0:T(8,128)(2,1)} %collective-permute-done.31.refs_19_), channel_id=1, source_target_pairs={{0,8},{4,12},{8,0},{12,4},{16,24},{20,28},{24,16},{28,20},{1,9},{5... | collective-permute-start | bytes 3145736 | tf_op jit(solution)/shard_map/ppermute | solution.py:207
  104.0 2.0 collective-permute-start.7
  107.0 48.6 %collective-permute-done.7 = bf16[2,48,2048]{2,1,0:T(8,128)(2,1)S(1)} collective-permute-done((bf16[2,48,2048]{2,1,0:T(8,128)(2,1)S(1)}, bf16[2,48,2048]{2,1,0:T(8,128)(2,1)S(1)}, u32[]{:S(2)}, u32[]{:S(2)}) %collective-permute-start.7) | collective-permute-done | bytes 393248 | tf_op jit(solution)/shard_map/ppermute | solution.py:211
  157.1 2.4 collective-permute-start.10
  159.5 1.7 collective-permute-start.24
  161.2 22.8 %collective-permute-done.25.refs_12_ = bf16[96,2048]{1,0:T(8,128)(2,1)S(1)} collective-permute-done((bf16[96,2048]{1,0:T(8,128)(2,1)S(1)}, bf16[96,2048]{1,0:T(8,128)(2,1)S(1)}, u32[]{:S(2)}, u32[]{:S(2)}) %collective-permute-start.25) | collective-permute-done | bytes 393248 | tf_op jit(solution)/shard_map/ppermute | solution.py:220
  186.0 6.5 %collective-permute-done.10.refs_4_ = bf16[96,2048]{1,0:T(8,128)(2,1)} collective-permute-done((bf16[96,2048]{1,0:T(8,128)(2,1)S(1)}, bf16[96,2048]{1,0:T(8,128)(2,1)}, u32[]{:S(2)}, u32[]{:S(2)}) %collective-permute-start.10) | collective-permute-done | bytes 393248 | tf_op jit(solution)/shard_map/ppermute | solution.py:220
  195.6 8.9 %collective-permute-done.9.refs_3_ = bf16[96,2048]{1,0:T(8,128)(2,1)} collective-permute-done((bf16[96,2048]{1,0:T(8,128)(2,1)S(1)}, bf16[96,2048]{1,0:T(8,128)(2,1)}, u32[]{:S(2)}, u32[]{:S(2)}) %collective-permute-start.9) | collective-permute-done | bytes 393248 | tf_op jit(solution)/shard_map/ppermute | solution.py:207
  204.5 4.2 %collective-permute-done.11.refs_5_ = bf16[96,2048]{1,0:T(8,128)(2,1)} collective-permute-done((bf16[96,2048]{1,0:T(8,128)(2,1)}, bf16[96,2048]{1,0:T(8,128)(2,1)}, u32[]{:S(2)}, u32[]{:S(2)}) %collective-permute-start.11) | collective-permute-done | bytes 393248 | tf_op jit(solution)/shard_map/ppermute | solution.py:207
  212.0 13.4 %finish.1 = f32[8,512]{1,0:T(8,128)} custom-call(s32[5]{0:T(128)} %stack.96.where_ref, f32[2,1,2048]{2,1,0:T(1,128)} %broadcast_in_dim.154.gain_in, bf16[16,256]{1,0:T(8,128)(2,1)} %copy-done.14, bf16[16,256]{1,0:T(8,128)(2,1)} %copy-done.15, bf16[96,2048]{1,0:T(8,128)(2,1)} %copy-done.7, bf16[96,2048]{1,0:T(8,128)(2,1)} %collective-permute-done.9.refs_3_, ...), custom_call_target="tpu_custom_call" | custom-call | tf_op jit(solution)/shard_map/finish/pallas_call | solution.py:157
  225.4 5.4 %all-gather = f32[32,512]{1,0:T(8,128)S(1)} all-gather(f32[8,512]{1,0:T(8,128)} %finish.1), channel_id=2, replica_groups=mesh['expert'=8,'vocab'=4] {'vocab'}, dimensions={0}, use_global_device_ids=true | all-gather | bytes 81920 | tf_op jit(solution)/shard_map/all_gather | solution.py:331
  231.7 12.6 %all_to_all.5 = f32[8,5,256]{2,1,0:T(8,128)S(1)} all-to-all(f32[8,5,256]{2,1,0:T(8,128)S(1)} %constant_dynamic-update-slice_fusion), channel_id=1, replica_groups=mesh['expert'=8,'vocab'=4] {'expert'}, dimensions={0} | all-to-all | bytes 81920 | tf_op jit(solution)/shard_map/all_to_all | solution.py:339
  (153 shorter events, 30.5 us)
Async XLA Ops:
  7.6 26.7 %collective-permute-start.16 = (bf16[48,2048]{1,0:T(8,128)(2,1)S(1)}, bf16[48,2048]{1,0:T(8,128)(2,1)S(1)}, u32[]{:S(2)}, u32[]{:S(2)}) collective-permute-start(bf16[48,2048]{1,0:T(8,128)(2,1)S(1)} %get-tuple-element.23), channel_id=1, source_target_pairs={{0,16},{4,20},{8,24},{12,28},{16,0},{20,4},{24,8},{28,12},{1,17},{... | collective-permute-start | bytes 589832 | tf_op jit(solution)/shard_map/ppermute | solution.py:207
  11.7 28.1 %collective-permute-start.17 = (bf16[48,2048]{1,0:T(8,128)(2,1)S(1)}, bf16[48,2048]{1,0:T(8,128)(2,1)S(1)}, u32[]{:S(2)}, u32[]{:S(2)}) collective-permute-start(bf16[48,2048]{1,0:T(8,128)(2,1)S(1)} %get-tuple-element.26), channel_id=1, source_target_pairs={{0,20},{4,16},{8,28},{12,24},{16,4},{20,0},{24,12},{28,8},{1,21},{... | collective-permute-start | bytes 589832 | tf_op jit(solution)/shard_map/ppermute | solution.py:207
  13.0 26.8 %collective-permute-start.18 = (bf16[48,2048]{1,0:T(8,128)(2,1)S(1)}, bf16[48,2048]{1,0:T(8,128)(2,1)S(1)}, u32[]{:S(2)}, u32[]{:S(2)}) collective-permute-start(bf16[48,2048]{1,0:T(8,128)(2,1)S(1)} %get-tuple-element.25), channel_id=1, source_target_pairs={{0,24},{4,28},{8,16},{12,20},{16,8},{20,12},{24,0},{28,4},{1,25},{... | collective-permute-start | bytes 589832 | tf_op jit(solution)/shard_map/ppermute | solution.py:207
  16.6 24.7 %collective-permute-start.19 = (bf16[48,2048]{1,0:T(8,128)(2,1)S(1)}, bf16[48,2048]{1,0:T(8,128)(2,1)S(1)}, u32[]{:S(2)}, u32[]{:S(2)}) collective-permute-start(bf16[48,2048]{1,0:T(8,128)(2,1)S(1)} %get-tuple-element.24), channel_id=1, source_target_pairs={{0,28},{4,24},{8,20},{12,16},{16,12},{20,8},{24,4},{28,0},{1,29},{... | collective-permute-start | bytes 589832 | tf_op jit(solution)/shard_map/ppermute | solution.py:207
  16.6 25.1 %collective-permute-start.2 = (bf16[48,2048]{1,0:T(8,128)(2,1)S(1)}, bf16[48,2048]{1,0:T(8,128)(2,1)S(1)}, u32[]{:S(2)}, u32[]{:S(2)}) collective-permute-start(bf16[48,2048]{1,0:T(8,128)(2,1)S(1)} %get-tuple-element.29), channel_id=1, source_target_pairs={{0,4},{4,0},{8,12},{12,8},{16,20},{20,16},{24,28},{28,24},{1,5},{5... | collective-permute-start | bytes 589832 | tf_op jit(solution)/shard_map/ppermute | solution.py:207
  34.3 16.6 %collective-permute-start.3 = (bf16[48,2048]{1,0:T(8,128)(2,1)S(1)}, bf16[48,2048]{1,0:T(8,128)(2,1)S(1)}, u32[]{:S(2)}, u32[]{:S(2)}) collective-permute-start(bf16[48,2048]{1,0:T(8,128)(2,1)S(1)} %get-tuple-element.28), channel_id=1, source_target_pairs={{0,8},{4,12},{8,0},{12,4},{16,24},{20,28},{24,16},{28,20},{1,9},{5... | collective-permute-start | bytes 589832 | tf_op jit(solution)/shard_map/ppermute | solution.py:207
  39.8 58.5 %collective-permute-start.31 = (bf16[256,2048]{1,0:T(8,128)(2,1)}, bf16[256,2048]{1,0:T(8,128)(2,1)}, u32[]{:S(2)}, u32[]{:S(2)}) collective-permute-start(bf16[256,2048]{1,0:T(8,128)(2,1)} %refs_18_.1), channel_id=1, source_target_pairs={{0,2},{1,3},{2,0},{3,1},{4,6},{5,7},{6,4},{7,5},{8,10},{9,11},{10,... | collective-permute-start | bytes 3145736 | tf_op jit(solution)/shard_map/ppermute | solution.py:211
  41.7 64.5 %collective-permute-start.32 = (bf16[256,2048]{1,0:T(8,128)(2,1)}, bf16[256,2048]{1,0:T(8,128)(2,1)}, u32[]{:S(2)}, u32[]{:S(2)}) collective-permute-start(bf16[256,2048]{1,0:T(8,128)(2,1)} %refs_18_.1), channel_id=1, source_target_pairs={{0,8},{4,12},{8,0},{12,4},{16,24},{20,28},{24,16},{28,20},{1,9},{5... | collective-permute-start | bytes 3145736 | tf_op jit(solution)/shard_map/ppermute | solution.py:207
  50.9 52.5 %collective-permute-start.35 = (bf16[256,2048]{1,0:T(8,128)(2,1)}, bf16[256,2048]{1,0:T(8,128)(2,1)}, u32[]{:S(2)}, u32[]{:S(2)}) collective-permute-start(bf16[256,2048]{1,0:T(8,128)(2,1)} %refs_22_.1), channel_id=1, source_target_pairs={{0,8},{4,12},{8,0},{12,4},{16,24},{20,28},{24,16},{28,20},{1,9},{5... | collective-permute-start | bytes 3145736 | tf_op jit(solution)/shard_map/ppermute | solution.py:207
  51.1 14.4 %collective-permute-start.5 = (bf16[192,2048]{1,0:T(8,128)(2,1)S(1)}, bf16[192,2048]{1,0:T(8,128)(2,1)}, u32[]{:S(2)}, u32[]{:S(2)}) collective-permute-start(bf16[192,2048]{1,0:T(8,128)(2,1)S(1)} %bitcast.198), channel_id=1, source_target_pairs={{0,1},{1,0},{2,3},{3,2},{4,5},{5,4},{6,7},{7,6},{8,9},{9,8},{10,11... | collective-permute-start | bytes 2359304 | tf_op jit(solution)/shard_map/ppermute | solution.py:211
  65.1 16.6 %collective-permute-start.21 = (bf16[2,2,48,2048]{3,2,1,0:T(8,128)(2,1)}, bf16[2,2,48,2048]{3,2,1,0:T(8,128)(2,1)}, u32[]{:S(2)}, u32[]{:S(2)}) collective-permute-start(bf16[2,2,48,2048]{3,2,1,0:T(8,128)(2,1)} %dynamic-slice_bitcast_fusion), channel_id=1, source_target_pairs={{0,1},{1,0},{2,3},{3,2},{4,5},{5,4},{6,7},{7,6},{8,9},{9,8},{10,11... | collective-permute-start | bytes 2359304 | tf_op jit(solution)/shard_map/ppermute | solution.py:211
  87.4 16.6 %collective-permute-start.22 = (bf16[2,48,2048]{2,1,0:T(8,128)(2,1)S(1)}, bf16[2,48,2048]{2,1,0:T(8,128)(2,1)S(1)}, u32[]{:S(2)}, u32[]{:S(2)}) collective-permute-start(bf16[2,48,2048]{2,1,0:T(8,128)(2,1)S(1)} %fusion.45), channel_id=1, source_target_pairs={{0,2},{1,3},{2,0},{3,1},{4,6},{5,7},{6,4},{7,5},{8,10},{9,11},{10,... | collective-permute-start | bytes 1179656 | tf_op jit(solution)/shard_map/ppermute | solution.py:211
  96.8 59.5 %collective-permute-start.34 = (bf16[256,2048]{1,0:T(8,128)(2,1)}, bf16[256,2048]{1,0:T(8,128)(2,1)S(1)}, u32[]{:S(2)}, u32[]{:S(2)}) collective-permute-start(bf16[256,2048]{1,0:T(8,128)(2,1)} %refs_22_.1), channel_id=1, source_target_pairs={{0,2},{1,3},{2,0},{3,1},{4,6},{5,7},{6,4},{7,5},{8,10},{9,11},{10,... | collective-permute-start | bytes 3145736 | tf_op jit(solution)/shard_map/ppermute | solution.py:211
  98.3 58.7 %collective-permute-start.33 = (bf16[256,2048]{1,0:T(8,128)(2,1)}, bf16[256,2048]{1,0:T(8,128)(2,1)S(1)}, u32[]{:S(2)}, u32[]{:S(2)}) collective-permute-start(bf16[256,2048]{1,0:T(8,128)(2,1)} %collective-permute-done.31.refs_19_), channel_id=1, source_target_pairs={{0,8},{4,12},{8,0},{12,4},{16,24},{20,28},{24,16},{28,20},{1,9},{5... | collective-permute-start | bytes 3145736 | tf_op jit(solution)/shard_map/ppermute | solution.py:207
  103.5 82.0 %collective-permute-start.36 = (bf16[256,2048]{1,0:T(8,128)(2,1)}, bf16[256,2048]{1,0:T(8,128)(2,1)S(1)}, u32[]{:S(2)}, u32[]{:S(2)}) collective-permute-start(bf16[256,2048]{1,0:T(8,128)(2,1)} %collective-permute-done.35.refs_24_), channel_id=1, source_target_pairs={{0,2},{1,3},{2,0},{3,1},{4,6},{5,7},{6,4},{7,5},{8,10},{9,11},{10,... | collective-permute-start | bytes 3145736 | tf_op jit(solution)/shard_map/ppermute | solution.py:211
  104.0 51.5 %collective-permute-start.7 = (bf16[2,48,2048]{2,1,0:T(8,128)(2,1)S(1)}, bf16[2,48,2048]{2,1,0:T(8,128)(2,1)S(1)}, u32[]{:S(2)}, u32[]{:S(2)}) collective-permute-start(bf16[2,48,2048]{2,1,0:T(8,128)(2,1)S(1)} %fusion.44), channel_id=1, source_target_pairs={{0,2},{1,3},{2,0},{3,1},{4,6},{5,7},{6,4},{7,5},{8,10},{9,11},{10,... | collective-permute-start | bytes 1179656 | tf_op jit(solution)/shard_map/ppermute | solution.py:211
  106.3 53.2 %collective-permute-start.23 = (bf16[96,2048]{1,0:T(8,128)(2,1)S(1)}, bf16[96,2048]{1,0:T(8,128)(2,1)S(1)}, u32[]{:S(2)}, u32[]{:S(2)}) collective-permute-start(bf16[96,2048]{1,0:T(8,128)(2,1)S(1)} %bitcast.207), channel_id=1, source_target_pairs={{0,0},{1,8},{2,2},{3,10},{4,4},{5,12},{6,6},{7,14},{8,1},{9,9},{10... | collective-permute-start | bytes 1179656 | tf_op jit(solution)/shard_map/ppermute | solution.py:220
  155.6 28.4 %collective-permute-start.25 = (bf16[96,2048]{1,0:T(8,128)(2,1)S(1)}, bf16[96,2048]{1,0:T(8,128)(2,1)S(1)}, u32[]{:S(2)}, u32[]{:S(2)}) collective-permute-start(bf16[96,2048]{1,0:T(8,128)(2,1)S(1)} %bitcast.208), channel_id=1, source_target_pairs={{0,16},{1,24},{2,18},{3,26},{4,20},{5,28},{6,22},{7,30},{8,17},{9,... | collective-permute-start | bytes 1179656 | tf_op jit(solution)/shard_map/ppermute | solution.py:220
  156.4 29.1 %collective-permute-start.8 = (bf16[96,2048]{1,0:T(8,128)(2,1)S(1)}, bf16[96,2048]{1,0:T(8,128)(2,1)S(1)}, u32[]{:S(2)}, u32[]{:S(2)}) collective-permute-start(bf16[96,2048]{1,0:T(8,128)(2,1)S(1)} %bitcast.205), channel_id=1, source_target_pairs={{0,0},{1,8},{2,2},{3,10},{4,4},{5,12},{6,6},{7,14},{8,1},{9,9},{10... | collective-permute-start | bytes 1179656 | tf_op jit(solution)/shard_map/ppermute | solution.py:220
  157.1 35.3 %collective-permute-start.10 = (bf16[96,2048]{1,0:T(8,128)(2,1)S(1)}, bf16[96,2048]{1,0:T(8,128)(2,1)}, u32[]{:S(2)}, u32[]{:S(2)}) collective-permute-start(bf16[96,2048]{1,0:T(8,128)(2,1)S(1)} %bitcast.206), channel_id=1, source_target_pairs={{0,16},{1,24},{2,18},{3,26},{4,20},{5,28},{6,22},{7,30},{8,17},{9,... | collective-permute-start | bytes 1179656 | tf_op jit(solution)/shard_map/ppermute | solution.py:220
  159.5 34.4 %collective-permute-start.24 = (bf16[96,2048]{1,0:T(8,128)(2,1)S(1)}, bf16[96,2048]{1,0:T(8,128)(2,1)}, u32[]{:S(2)}, u32[]{:S(2)}) collective-permute-start(bf16[96,2048]{1,0:T(8,128)(2,1)S(1)} %collective-permute-done.23.refs_10_), channel_id=1, source_target_pairs={{0,4},{4,0},{8,12},{12,8},{16,20},{20,16},{24,28},{28,24},{1,5},{5... | collective-permute-start | bytes 1179656 | tf_op jit(solution)/shard_map/ppermute | solution.py:207
  193.9 14.8 %collective-permute-start.11 = (bf16[96,2048]{1,0:T(8,128)(2,1)}, bf16[96,2048]{1,0:T(8,128)(2,1)}, u32[]{:S(2)}, u32[]{:S(2)}) collective-permute-start(bf16[96,2048]{1,0:T(8,128)(2,1)} %collective-permute-done.10.refs_4_), channel_id=1, source_target_pairs={{0,4},{4,0},{8,12},{12,8},{16,20},{20,16},{24,28},{28,24},{1,5},{5... | collective-permute-start | bytes 1179656 | tf_op jit(solution)/shard_map/ppermute | solution.py:207
  194.9 17.0 %collective-permute-start.14 = (bf16[96,2048]{1,0:T(8,128)(2,1)}, bf16[96,2048]{1,0:T(8,128)(2,1)}, u32[]{:S(2)}, u32[]{:S(2)}) collective-permute-start(bf16[96,2048]{1,0:T(8,128)(2,1)} %collective-permute-done.10.refs_4_), channel_id=1, source_target_pairs={{0,1},{1,0},{2,3},{3,2},{4,5},{5,4},{6,7},{7,6},{8,9},{9,8},{10,11... | collective-permute-start | bytes 1179656 | tf_op jit(solution)/shard_map/ppermute | solution.py:211
  195.5 16.4 %collective-permute-start.28 = (bf16[96,2048]{1,0:T(8,128)(2,1)}, bf16[96,2048]{1,0:T(8,128)(2,1)}, u32[]{:S(2)}, u32[]{:S(2)}) collective-permute-start(bf16[96,2048]{1,0:T(8,128)(2,1)} %collective-permute-done.24.refs_11_), channel_id=1, source_target_pairs={{0,1},{1,0},{2,3},{3,2},{4,5},{5,4},{6,7},{7,6},{8,9},{9,8},{10,11... | collective-permute-start | bytes 1179656 | tf_op jit(solution)/shard_map/ppermute | solution.py:211
  (29 other events, 529.1 us)

commit v2 on v1

--- a/solution.py
+++ b/solution.py
@@ -133,12 +133,12 @@
         for branch in range(2):
             for i in range(counts[2] // 2):
                 copies["head", branch * (counts[2] // 2) + i].wait()
-            for t in range(rows // 512):
-                logits[branch, :, t*512:(t+1)*512] = lax.dot_general(
-                    head[branch], normed[branch, t*512:(t+1)*512, :],
-                    (((1,), (1,)), ((), ())),
-                    preferred_element_type=jnp.float32,
-                )
+            logits[branch] = lax.dot_general(
+                head[branch],
+                normed[branch],
+                (((1,), (1,)), ((), ())),
+                preferred_element_type=jnp.float32,
+            )
         for t in range(rows // 128):
             here = slice(t * 128, (t + 1) * 128)
             teacher, student = logits[0, :, here], logits[1, :, here]

time: 245 us -> 245 us (level)
  no operation moved by 1% of the time
where the time goes in v2:
time: 245 us
  waiting for transfers between devices  116 us (47%)
  starting transfers between devices  53.3 us (22%)
  matrix products  27.4 us (11%)
  blocking collectives  18 us (7%)
  Pallas kernels  13.4 us (5%)
  other arithmetic  12.7 us (5%)
  local copies, waits for them, and re-layouts  3.52 us (1%)
    ppermute x17, waiting for transfers between devices, by_vocab(): lax.ppermute(array, 'vocab', [pair for pair in perm if pair[1] is not None])  49.1 us
    ppermute x14, waiting for transfers between devices, by_expert(): return lax.ppermute(array, 'expert', [(s, move(s)) for s in range(En)])  35 us
    ppermute x6, waiting for transfers between devices, by_both(): return lax.ppermute(array, BOTH, perm)  31.8 us
    ppermute x14, starting transfers between devices, by_expert(): return lax.ppermute(array, 'expert', [(s, move(s)) for s in range(En)])  30.2 us
    dot_general x2, matrix products, ffn(): jnp.dot(hidden, weight_out, preferred_element_type=jnp.float32)  25.6 us
    ppermute x17, starting transfers between devices, by_vocab(): lax.ppermute(array, 'vocab', [pair for pair in perm if pair[1] is not None])  14.5 us
    pallas_call x1, Pallas kernels, finish(): pl.pallas_call(kernel, in_specs=[pl.BlockSpec(memory_space=pltpu.SMEM)] +...  13.4 us
    all_to_all x1, blocking collectives, local(): lax.all_to_all(jnp.stack(letters), 'expert', split_axis=0, concat_axis=0,...  12.6 us
  transfers between devices with their start and end apart: 37, of which 10 were waited for; matrix products, arithmetic and copies ran while one was open for 14% of the time, Pallas kernels for 0%

profile of v2, /device:TPU:0, one launch (start us, length us, event | category | flops | bytes accessed | tf_op | source)
XLA Modules:
  0.0 244.9 jit_solution(13484920914629447563)
XLA Ops:
  5.6 1.8 convolution_convert_fusion
  7.6 4.1 %collective-permute-start.16 = (bf16[48,2048]{1,0:T(8,128)(2,1)S(1)}, bf16[48,2048]{1,0:T(8,128)(2,1)S(1)}, u32[]{:S(2)}, u32[]{:S(2)}) collective-permute-start(bf16[48,2048]{1,0:T(8,128)(2,1)S(1)} %get-tuple-element.23), channel_id=1, source_target_pairs={{0,16},{4,20},{8,24},{12,28},{16,0},{20,4},{24,8},{28,12},{1,17},{... | collective-permute-start | bytes 589832 | tf_op jit(solution)/shard_map/ppermute | solution.py:207
  13.0 3.6 %collective-permute-start.18 = (bf16[48,2048]{1,0:T(8,128)(2,1)S(1)}, bf16[48,2048]{1,0:T(8,128)(2,1)S(1)}, u32[]{:S(2)}, u32[]{:S(2)}) collective-permute-start(bf16[48,2048]{1,0:T(8,128)(2,1)S(1)} %get-tuple-element.25), channel_id=1, source_target_pairs={{0,24},{4,28},{8,16},{12,20},{16,8},{20,12},{24,0},{28,4},{1,25},{... | collective-permute-start | bytes 589832 | tf_op jit(solution)/shard_map/ppermute | solution.py:207
  16.6 1.7 collective-permute-start.2
  18.3 16.0 %collective-permute-done.16 = bf16[48,2048]{1,0:T(8,128)(2,1)S(1)} collective-permute-done((bf16[48,2048]{1,0:T(8,128)(2,1)S(1)}, bf16[48,2048]{1,0:T(8,128)(2,1)S(1)}, u32[]{:S(2)}, u32[]{:S(2)}) %collective-permute-start.16) | collective-permute-done | bytes 196640 | tf_op jit(solution)/shard_map/ppermute | solution.py:207
  34.3 5.5 %collective-permute-done.17 = bf16[48,2048]{1,0:T(8,128)(2,1)S(1)} collective-permute-done((bf16[48,2048]{1,0:T(8,128)(2,1)S(1)}, bf16[48,2048]{1,0:T(8,128)(2,1)S(1)}, u32[]{:S(2)}, u32[]{:S(2)}) %collective-permute-start.17) | collective-permute-done | bytes 196640 | tf_op jit(solution)/shard_map/ppermute | solution.py:207
  41.7 9.2 %collective-permute-start.32 = (bf16[256,2048]{1,0:T(8,128)(2,1)}, bf16[256,2048]{1,0:T(8,128)(2,1)}, u32[]{:S(2)}, u32[]{:S(2)}) collective-permute-start(bf16[256,2048]{1,0:T(8,128)(2,1)} %refs_18_.1), channel_id=1, source_target_pairs={{0,8},{4,12},{8,0},{12,4},{16,24},{20,28},{24,16},{28,20},{1,9},{5... | collective-permute-start | bytes 3145736 | tf_op jit(solution)/shard_map/ppermute | solution.py:207
  51.4 12.7 %fusion.27 = bf16[384,2048]{1,0:T(8,128)(2,1)S(1)} fusion(bf16[1,2048,2048]{2,1,0:T(8,128)(2,1)} %param.16, bf16[1,2048,2048]{2,1,0:T(8,128)(2,1)} %param.15, bf16[192,2048]{1,0:T(8,128)(2,1)} %collective-permute-done.20, bf16[192,2048]{1,0:T(8,128)(2,1)S(1)} %bitcast.196), kind=kOutput, calls=%fused_computation.27 | convolution fusion | flops 6453460992 | bytes 19922944 | tf_op jit(solution)/shard_map/dot_general | solution.py:38
  65.5 12.9 %fusion.24 = bf16[384,2048]{1,0:T(8,128)(2,1)S(1)} fusion(bf16[1,2048,2048]{2,1,0:T(8,128)(2,1)} %param.16, bf16[1,2048,2048]{2,1,0:T(8,128)(2,1)} %param.15, bf16[192,2048]{1,0:T(8,128)(2,1)} %collective-permute-done.5, bf16[192,2048]{1,0:T(8,128)(2,1)S(1)} %bitcast.199), kind=kOutput, calls=%fused_computation.26 | convolution fusion | flops 6453460992 | bytes 19922944 | tf_op jit(solution)/shard_map/dot_general | solution.py:38
  83.8 3.6 %collective-permute-start.1 = (bf16[16,256]{1,0:T(8,128)(2,1)S(1)}, bf16[16,256]{1,0:T(8,128)(2,1)S(1)}, u32[]{:S(2)}, u32[]{:S(2)}) collective-permute-start(bf16[16,256]{1,0:T(8,128)(2,1)S(1)} %pad.4), channel_id=1, source_target_pairs={{0,16},{1,17},{2,20},{3,21},{4,18},{5,19},{6,22},{7,23},{8,24},{9,... | collective-permute-start | bytes 24584 | tf_op jit(solution)/shard_map/ppermute | solution.py:220
  87.4 6.6 %collective-permute-start.22 = (bf16[2,48,2048]{2,1,0:T(8,128)(2,1)S(1)}, bf16[2,48,2048]{2,1,0:T(8,128)(2,1)S(1)}, u32[]{:S(2)}, u32[]{:S(2)}) collective-permute-start(bf16[2,48,2048]{2,1,0:T(8,128)(2,1)S(1)} %fusion.45), channel_id=1, source_target_pairs={{0,2},{1,3},{2,0},{3,1},{4,6},{5,7},{6,4},{7,5},{8,10},{9,11},{10,... | collective-permute-start | bytes 1179656 | tf_op jit(solution)/shard_map/ppermute | solution.py:211
  94.3 2.6 %collective-permute-done.1.refs_1_ = bf16[16,256]{1,0:T(8,128)(2,1)S(1)} collective-permute-done((bf16[16,256]{1,0:T(8,128)(2,1)S(1)}, bf16[16,256]{1,0:T(8,128)(2,1)S(1)}, u32[]{:S(2)}, u32[]{:S(2)}) %collective-permute-start.1) | collective-permute-done | bytes 8224 | tf_op jit(solution)/shard_map/ppermute | solution.py:220
  98.3 5.1 %collective-permute-start.33 = (bf16[256,2048]{1,0:T(8,128)(2,1)}, bf16[256,2048]{1,0:T(8,128)(2,1)S(1)}, u32[]{:S(2)}, u32[]{:S(2)}) collective-permute-start(bf16[256,2048]{1,0:T(8,128)(2,1)} %collective-permute-done.31.refs_19_), channel_id=1, source_target_pairs={{0,8},{4,12},{8,0},{12,4},{16,24},{20,28},{24,16},{28,20},{1,9},{5... | collective-permute-start | bytes 3145736 | tf_op jit(solution)/shard_map/ppermute | solution.py:207
  104.0 2.0 collective-permute-start.7
  107.0 48.6 %collective-permute-done.7 = bf16[2,48,2048]{2,1,0:T(8,128)(2,1)S(1)} collective-permute-done((bf16[2,48,2048]{2,1,0:T(8,128)(2,1)S(1)}, bf16[2,48,2048]{2,1,0:T(8,128)(2,1)S(1)}, u32[]{:S(2)}, u32[]{:S(2)}) %collective-permute-start.7) | collective-permute-done | bytes 393248 | tf_op jit(solution)/shard_map/ppermute | solution.py:211
  157.1 2.4 collective-permute-start.10
  159.5 1.7 collective-permute-start.24
  161.2 22.8 %collective-permute-done.25.refs_12_ = bf16[96,2048]{1,0:T(8,128)(2,1)S(1)} collective-permute-done((bf16[96,2048]{1,0:T(8,128)(2,1)S(1)}, bf16[96,2048]{1,0:T(8,128)(2,1)S(1)}, u32[]{:S(2)}, u32[]{:S(2)}) %collective-permute-start.25) | collective-permute-done | bytes 393248 | tf_op jit(solution)/shard_map/ppermute | solution.py:220
  186.0 6.5 %collective-permute-done.10.refs_4_ = bf16[96,2048]{1,0:T(8,128)(2,1)} collective-permute-done((bf16[96,2048]{1,0:T(8,128)(2,1)S(1)}, bf16[96,2048]{1,0:T(8,128)(2,1)}, u32[]{:S(2)}, u32[]{:S(2)}) %collective-permute-start.10) | collective-permute-done | bytes 393248 | tf_op jit(solution)/shard_map/ppermute | solution.py:220
  195.6 8.9 %collective-permute-done.9.refs_3_ = bf16[96,2048]{1,0:T(8,128)(2,1)} collective-permute-done((bf16[96,2048]{1,0:T(8,128)(2,1)S(1)}, bf16[96,2048]{1,0:T(8,128)(2,1)}, u32[]{:S(2)}, u32[]{:S(2)}) %collective-permute-start.9) | collective-permute-done | bytes 393248 | tf_op jit(solution)/shard_map/ppermute | solution.py:207
  204.5 4.2 %collective-permute-done.11.refs_5_ = bf16[96,2048]{1,0:T(8,128)(2,1)} collective-permute-done((bf16[96,2048]{1,0:T(8,128)(2,1)}, bf16[96,2048]{1,0:T(8,128)(2,1)}, u32[]{:S(2)}, u32[]{:S(2)}) %collective-permute-start.11) | collective-permute-done | bytes 393248 | tf_op jit(solution)/shard_map/ppermute | solution.py:207
  212.0 13.4 %finish.1 = f32[8,512]{1,0:T(8,128)} custom-call(s32[5]{0:T(128)} %stack.96.where_ref, f32[2,1,2048]{2,1,0:T(1,128)} %broadcast_in_dim.154.gain_in, bf16[16,256]{1,0:T(8,128)(2,1)} %copy-done.14, bf16[16,256]{1,0:T(8,128)(2,1)} %copy-done.15, bf16[96,2048]{1,0:T(8,128)(2,1)} %copy-done.7, bf16[96,2048]{1,0:T(8,128)(2,1)} %collective-permute-done.9.refs_3_, ...), custom_call_target="tpu_custom_call" | custom-call | tf_op jit(solution)/shard_map/finish/pallas_call | solution.py:157
  225.4 5.4 %all-gather = f32[32,512]{1,0:T(8,128)S(1)} all-gather(f32[8,512]{1,0:T(8,128)} %finish.1), channel_id=2, replica_groups=mesh['expert'=8,'vocab'=4] {'vocab'}, dimensions={0}, use_global_device_ids=true | all-gather | bytes 81920 | tf_op jit(solution)/shard_map/all_gather | solution.py:331
  231.7 12.6 %all_to_all.5 = f32[8,5,256]{2,1,0:T(8,128)S(1)} all-to-all(f32[8,5,256]{2,1,0:T(8,128)S(1)} %constant_dynamic-update-slice_fusion), channel_id=1, replica_groups=mesh['expert'=8,'vocab'=4] {'expert'}, dimensions={0} | all-to-all | bytes 81920 | tf_op jit(solution)/shard_map/all_to_all | solution.py:339
  (153 shorter events, 30.5 us)
Async XLA Ops:
  7.6 26.7 %collective-permute-start.16 = (bf16[48,2048]{1,0:T(8,128)(2,1)S(1)}, bf16[48,2048]{1,0:T(8,128)(2,1)S(1)}, u32[]{:S(2)}, u32[]{:S(2)}) collective-permute-start(bf16[48,2048]{1,0:T(8,128)(2,1)S(1)} %get-tuple-element.23), channel_id=1, source_target_pairs={{0,16},{4,20},{8,24},{12,28},{16,0},{20,4},{24,8},{28,12},{1,17},{... | collective-permute-start | bytes 589832 | tf_op jit(solution)/shard_map/ppermute | solution.py:207
  11.7 28.1 %collective-permute-start.17 = (bf16[48,2048]{1,0:T(8,128)(2,1)S(1)}, bf16[48,2048]{1,0:T(8,128)(2,1)S(1)}, u32[]{:S(2)}, u32[]{:S(2)}) collective-permute-start(bf16[48,2048]{1,0:T(8,128)(2,1)S(1)} %get-tuple-element.26), channel_id=1, source_target_pairs={{0,20},{4,16},{8,28},{12,24},{16,4},{20,0},{24,12},{28,8},{1,21},{... | collective-permute-start | bytes 589832 | tf_op jit(solution)/shard_map/ppermute | solution.py:207
  13.0 26.8 %collective-permute-start.18 = (bf16[48,2048]{1,0:T(8,128)(2,1)S(1)}, bf16[48,2048]{1,0:T(8,128)(2,1)S(1)}, u32[]{:S(2)}, u32[]{:S(2)}) collective-permute-start(bf16[48,2048]{1,0:T(8,128)(2,1)S(1)} %get-tuple-element.25), channel_id=1, source_target_pairs={{0,24},{4,28},{8,16},{12,20},{16,8},{20,12},{24,0},{28,4},{1,25},{... | collective-permute-start | bytes 589832 | tf_op jit(solution)/shard_map/ppermute | solution.py:207
  16.6 24.7 %collective-permute-start.19 = (bf16[48,2048]{1,0:T(8,128)(2,1)S(1)}, bf16[48,2048]{1,0:T(8,128)(2,1)S(1)}, u32[]{:S(2)}, u32[]{:S(2)}) collective-permute-start(bf16[48,2048]{1,0:T(8,128)(2,1)S(1)} %get-tuple-element.24), channel_id=1, source_target_pairs={{0,28},{4,24},{8,20},{12,16},{16,12},{20,8},{24,4},{28,0},{1,29},{... | collective-permute-start | bytes 589832 | tf_op jit(solution)/shard_map/ppermute | solution.py:207
  16.6 25.1 %collective-permute-start.2 = (bf16[48,2048]{1,0:T(8,128)(2,1)S(1)}, bf16[48,2048]{1,0:T(8,128)(2,1)S(1)}, u32[]{:S(2)}, u32[]{:S(2)}) collective-permute-start(bf16[48,2048]{1,0:T(8,128)(2,1)S(1)} %get-tuple-element.29), channel_id=1, source_target_pairs={{0,4},{4,0},{8,12},{12,8},{16,20},{20,16},{24,28},{28,24},{1,5},{5... | collective-permute-start | bytes 589832 | tf_op jit(solution)/shard_map/ppermute | solution.py:207
  34.3 16.6 %collective-permute-start.3 = (bf16[48,2048]{1,0:T(8,128)(2,1)S(1)}, bf16[48,2048]{1,0:T(8,128)(2,1)S(1)}, u32[]{:S(2)}, u32[]{:S(2)}) collective-permute-start(bf16[48,2048]{1,0:T(8,128)(2,1)S(1)} %get-tuple-element.28), channel_id=1, source_target_pairs={{0,8},{4,12},{8,0},{12,4},{16,24},{20,28},{24,16},{28,20},{1,9},{5... | collective-permute-start | bytes 589832 | tf_op jit(solution)/shard_map/ppermute | solution.py:207
  39.8 58.5 %collective-permute-start.31 = (bf16[256,2048]{1,0:T(8,128)(2,1)}, bf16[256,2048]{1,0:T(8,128)(2,1)}, u32[]{:S(2)}, u32[]{:S(2)}) collective-permute-start(bf16[256,2048]{1,0:T(8,128)(2,1)} %refs_18_.1), channel_id=1, source_target_pairs={{0,2},{1,3},{2,0},{3,1},{4,6},{5,7},{6,4},{7,5},{8,10},{9,11},{10,... | collective-permute-start | bytes 3145736 | tf_op jit(solution)/shard_map/ppermute | solution.py:211
  41.7 64.5 %collective-permute-start.32 = (bf16[256,2048]{1,0:T(8,128)(2,1)}, bf16[256,2048]{1,0:T(8,128)(2,1)}, u32[]{:S(2)}, u32[]{:S(2)}) collective-permute-start(bf16[256,2048]{1,0:T(8,128)(2,1)} %refs_18_.1), channel_id=1, source_target_pairs={{0,8},{4,12},{8,0},{12,4},{16,24},{20,28},{24,16},{28,20},{1,9},{5... | collective-permute-start | bytes 3145736 | tf_op jit(solution)/shard_map/ppermute | solution.py:207
  50.9 52.5 %collective-permute-start.35 = (bf16[256,2048]{1,0:T(8,128)(2,1)}, bf16[256,2048]{1,0:T(8,128)(2,1)}, u32[]{:S(2)}, u32[]{:S(2)}) collective-permute-start(bf16[256,2048]{1,0:T(8,128)(2,1)} %refs_22_.1), channel_id=1, source_target_pairs={{0,8},{4,12},{8,0},{12,4},{16,24},{20,28},{24,16},{28,20},{1,9},{5... | collective-permute-start | bytes 3145736 | tf_op jit(solution)/shard_map/ppermute | solution.py:207
  51.1 14.4 %collective-permute-start.5 = (bf16[192,2048]{1,0:T(8,128)(2,1)S(1)}, bf16[192,2048]{1,0:T(8,128)(2,1)}, u32[]{:S(2)}, u32[]{:S(2)}) collective-permute-start(bf16[192,2048]{1,0:T(8,128)(2,1)S(1)} %bitcast.198), channel_id=1, source_target_pairs={{0,1},{1,0},{2,3},{3,2},{4,5},{5,4},{6,7},{7,6},{8,9},{9,8},{10,11... | collective-permute-start | bytes 2359304 | tf_op jit(solution)/shard_map/ppermute | solution.py:211
  65.1 16.6 %collective-permute-start.21 = (bf16[2,2,48,2048]{3,2,1,0:T(8,128)(2,1)}, bf16[2,2,48,2048]{3,2,1,0:T(8,128)(2,1)}, u32[]{:S(2)}, u32[]{:S(2)}) collective-permute-start(bf16[2,2,48,2048]{3,2,1,0:T(8,128)(2,1)} %dynamic-slice_bitcast_fusion), channel_id=1, source_target_pairs={{0,1},{1,0},{2,3},{3,2},{4,5},{5,4},{6,7},{7,6},{8,9},{9,8},{10,11... | collective-permute-start | bytes 2359304 | tf_op jit(solution)/shard_map/ppermute | solution.py:211
  87.4 16.6 %collective-permute-start.22 = (bf16[2,48,2048]{2,1,0:T(8,128)(2,1)S(1)}, bf16[2,48,2048]{2,1,0:T(8,128)(2,1)S(1)}, u32[]{:S(2)}, u32[]{:S(2)}) collective-permute-start(bf16[2,48,2048]{2,1,0:T(8,128)(2,1)S(1)} %fusion.45), channel_id=1, source_target_pairs={{0,2},{1,3},{2,0},{3,1},{4,6},{5,7},{6,4},{7,5},{8,10},{9,11},{10,... | collective-permute-start | bytes 1179656 | tf_op jit(solution)/shard_map/ppermute | solution.py:211
  96.8 59.5 %collective-permute-start.34 = (bf16[256,2048]{1,0:T(8,128)(2,1)}, bf16[256,2048]{1,0:T(8,128)(2,1)S(1)}, u32[]{:S(2)}, u32[]{:S(2)}) collective-permute-start(bf16[256,2048]{1,0:T(8,128)(2,1)} %refs_22_.1), channel_id=1, source_target_pairs={{0,2},{1,3},{2,0},{3,1},{4,6},{5,7},{6,4},{7,5},{8,10},{9,11},{10,... | collective-permute-start | bytes 3145736 | tf_op jit(solution)/shard_map/ppermute | solution.py:211
  98.3 58.7 %collective-permute-start.33 = (bf16[256,2048]{1,0:T(8,128)(2,1)}, bf16[256,2048]{1,0:T(8,128)(2,1)S(1)}, u32[]{:S(2)}, u32[]{:S(2)}) collective-permute-start(bf16[256,2048]{1,0:T(8,128)(2,1)} %collective-permute-done.31.refs_19_), channel_id=1, source_target_pairs={{0,8},{4,12},{8,0},{12,4},{16,24},{20,28},{24,16},{28,20},{1,9},{5... | collective-permute-start | bytes 3145736 | tf_op jit(solution)/shard_map/ppermute | solution.py:207
  103.5 82.0 %collective-permute-start.36 = (bf16[256,2048]{1,0:T(8,128)(2,1)}, bf16[256,2048]{1,0:T(8,128)(2,1)S(1)}, u32[]{:S(2)}, u32[]{:S(2)}) collective-permute-start(bf16[256,2048]{1,0:T(8,128)(2,1)} %collective-permute-done.35.refs_24_), channel_id=1, source_target_pairs={{0,2},{1,3},{2,0},{3,1},{4,6},{5,7},{6,4},{7,5},{8,10},{9,11},{10,... | collective-permute-start | bytes 3145736 | tf_op jit(solution)/shard_map/ppermute | solution.py:211
  104.0 51.5 %collective-permute-start.7 = (bf16[2,48,2048]{2,1,0:T(8,128)(2,1)S(1)}, bf16[2,48,2048]{2,1,0:T(8,128)(2,1)S(1)}, u32[]{:S(2)}, u32[]{:S(2)}) collective-permute-start(bf16[2,48,2048]{2,1,0:T(8,128)(2,1)S(1)} %fusion.44), channel_id=1, source_target_pairs={{0,2},{1,3},{2,0},{3,1},{4,6},{5,7},{6,4},{7,5},{8,10},{9,11},{10,... | collective-permute-start | bytes 1179656 | tf_op jit(solution)/shard_map/ppermute | solution.py:211
  106.3 53.2 %collective-permute-start.23 = (bf16[96,2048]{1,0:T(8,128)(2,1)S(1)}, bf16[96,2048]{1,0:T(8,128)(2,1)S(1)}, u32[]{:S(2)}, u32[]{:S(2)}) collective-permute-start(bf16[96,2048]{1,0:T(8,128)(2,1)S(1)} %bitcast.207), channel_id=1, source_target_pairs={{0,0},{1,8},{2,2},{3,10},{4,4},{5,12},{6,6},{7,14},{8,1},{9,9},{10... | collective-permute-start | bytes 1179656 | tf_op jit(solution)/shard_map/ppermute | solution.py:220
  155.6 28.4 %collective-permute-start.25 = (bf16[96,2048]{1,0:T(8,128)(2,1)S(1)}, bf16[96,2048]{1,0:T(8,128)(2,1)S(1)}, u32[]{:S(2)}, u32[]{:S(2)}) collective-permute-start(bf16[96,2048]{1,0:T(8,128)(2,1)S(1)} %bitcast.208), channel_id=1, source_target_pairs={{0,16},{1,24},{2,18},{3,26},{4,20},{5,28},{6,22},{7,30},{8,17},{9,... | collective-permute-start | bytes 1179656 | tf_op jit(solution)/shard_map/ppermute | solution.py:220
  156.4 29.1 %collective-permute-start.8 = (bf16[96,2048]{1,0:T(8,128)(2,1)S(1)}, bf16[96,2048]{1,0:T(8,128)(2,1)S(1)}, u32[]{:S(2)}, u32[]{:S(2)}) collective-permute-start(bf16[96,2048]{1,0:T(8,128)(2,1)S(1)} %bitcast.205), channel_id=1, source_target_pairs={{0,0},{1,8},{2,2},{3,10},{4,4},{5,12},{6,6},{7,14},{8,1},{9,9},{10... | collective-permute-start | bytes 1179656 | tf_op jit(solution)/shard_map/ppermute | solution.py:220
  157.1 35.3 %collective-permute-start.10 = (bf16[96,2048]{1,0:T(8,128)(2,1)S(1)}, bf16[96,2048]{1,0:T(8,128)(2,1)}, u32[]{:S(2)}, u32[]{:S(2)}) collective-permute-start(bf16[96,2048]{1,0:T(8,128)(2,1)S(1)} %bitcast.206), channel_id=1, source_target_pairs={{0,16},{1,24},{2,18},{3,26},{4,20},{5,28},{6,22},{7,30},{8,17},{9,... | collective-permute-start | bytes 1179656 | tf_op jit(solution)/shard_map/ppermute | solution.py:220
  159.5 34.4 %collective-permute-start.24 = (bf16[96,2048]{1,0:T(8,128)(2,1)S(1)}, bf16[96,2048]{1,0:T(8,128)(2,1)}, u32[]{:S(2)}, u32[]{:S(2)}) collective-permute-start(bf16[96,2048]{1,0:T(8,128)(2,1)S(1)} %collective-permute-done.23.refs_10_), channel_id=1, source_target_pairs={{0,4},{4,0},{8,12},{12,8},{16,20},{20,16},{24,28},{28,24},{1,5},{5... | collective-permute-start | bytes 1179656 | tf_op jit(solution)/shard_map/ppermute | solution.py:207
  193.9 14.8 %collective-permute-start.11 = (bf16[96,2048]{1,0:T(8,128)(2,1)}, bf16[96,2048]{1,0:T(8,128)(2,1)}, u32[]{:S(2)}, u32[]{:S(2)}) collective-permute-start(bf16[96,2048]{1,0:T(8,128)(2,1)} %collective-permute-done.10.refs_4_), channel_id=1, source_target_pairs={{0,4},{4,0},{8,12},{12,8},{16,20},{20,16},{24,28},{28,24},{1,5},{5... | collective-permute-start | bytes 1179656 | tf_op jit(solution)/shard_map/ppermute | solution.py:207
  194.9 17.0 %collective-permute-start.14 = (bf16[96,2048]{1,0:T(8,128)(2,1)}, bf16[96,2048]{1,0:T(8,128)(2,1)}, u32[]{:S(2)}, u32[]{:S(2)}) collective-permute-start(bf16[96,2048]{1,0:T(8,128)(2,1)} %collective-permute-done.10.refs_4_), channel_id=1, source_target_pairs={{0,1},{1,0},{2,3},{3,2},{4,5},{5,4},{6,7},{7,6},{8,9},{9,8},{10,11... | collective-permute-start | bytes 1179656 | tf_op jit(solution)/shard_map/ppermute | solution.py:211
  195.5 16.4 %collective-permute-start.28 = (bf16[96,2048]{1,0:T(8,128)(2,1)}, bf16[96,2048]{1,0:T(8,128)(2,1)}, u32[]{:S(2)}, u32[]{:S(2)}) collective-permute-start(bf16[96,2048]{1,0:T(8,128)(2,1)} %collective-permute-done.24.refs_11_), channel_id=1, source_target_pairs={{0,1},{1,0},{2,3},{3,2},{4,5},{5,4},{6,7},{7,6},{8,9},{9,8},{10,11... | collective-permute-start | bytes 1179656 | tf_op jit(solution)/shard_map/ppermute | solution.py:211
  (29 other events, 529.1 us)
